TPU v7x, 64 devices: a 2x2x8 block of a 4x4x8 slice. The times are simulated.
64 devices in a mesh: rep: 4 (over x, y), dp: 16 (over z, core).
Axes of the slice: x: 2, y: 2, z: 8, core: 2. Of those that a mesh axis runs over, the one named last changes fastest.
The devices are a block of a 4x4x8 slice.
Arguments:
- g_w_gate: bfloat16 [64, 2, 896, 2560], P(('rep', 'dp')), parts along dimension 0
- g_w_up: bfloat16 [64, 2, 896, 2560], P(('rep', 'dp')), parts along dimension 0
- g_w_down: bfloat16 [64, 2, 2560, 896], P(('rep', 'dp')), parts along dimension 0
- w_gate: bfloat16 [2, 896, 2560], replicated
- w_up: bfloat16 [2, 896, 2560], replicated
- w_down: bfloat16 [2, 2560, 896], replicated
- m_w_gate: float32 [2, 896, 2560], P(None, 'dp')
- m_w_up: float32 [2, 896, 2560], P(None, 'dp')
- m_w_down: float32 [2, 2560, 896], P(None, 'dp')
- v_w_gate: float32 [2, 896, 2560], P(None, 'dp')
- v_w_up: float32 [2, 896, 2560], P(None, 'dp')
- v_w_down: float32 [2, 2560, 896], P(None, 'dp')
Outputs:
- output 1: bfloat16 [8, 896, 2560], P('rep'), parts along dimension 0
- output 2: bfloat16 [8, 896, 2560], P('rep'), parts along dimension 0
- output 3: bfloat16 [8, 2560, 896], P('rep'), parts along dimension 0
- output 4: float32 [8, 896, 2560], P('rep', 'dp'), parts along dimension 0
- output 5: float32 [8, 896, 2560], P('rep', 'dp'), parts along dimension 0
- output 6: float32 [8, 2560, 896], P('rep', 'dp'), parts along dimension 0
- output 7: float32 [8, 896, 2560], P('rep', 'dp'), parts along dimension 0
- output 8: float32 [8, 896, 2560], P('rep', 'dp'), parts along dimension 0
- output 9: float32 [8, 2560, 896], P('rep', 'dp'), parts along dimension 0
There are 4 independent parts. A program takes and returns all parts, laid end to end along the dimension named above; an argument that names none is the same for every part.
All inputs are finite; a program needn't handle non-finite values.
Results may differ from a plain program's by a relative error of at most 0.022.
Values are sent between devices in bfloat16 or wider.
A program may use at most 768 MiB of HBM per device.

v0:
```python
import jax
import jax.numpy as jnp
from jax import lax
from jax.sharding import PartitionSpec as P


def adamw(w, m, v, g):
    m = 0.9 * m + 0.1 * g
    v = 0.95 * v + 0.05 * g * g
    step = m * lax.rsqrt(v + 1e-8) + 0.1 * w
    return (w - 0.02 * step).astype(jnp.bfloat16), m, v


def clipped(gradients, sum_of_squares, count):
    factor = jnp.minimum(1.0, 0.5 * lax.rsqrt(sum_of_squares / count + 1e-30))
    return [g * factor for g in gradients]


def solution(mesh):
    def step(*arrays):
        terms, weights, m, v = (arrays[i : i + 3] for i in (0, 3, 6, 9))
        gradients = [lax.psum_scatter(t[0], "dp", scatter_dimension=1, tiled=True).astype(jnp.float32) for t in terms]
        squares = lax.psum(sum(jnp.sum(g * g) for g in gradients), "dp")
        gradients = clipped(gradients, squares, lax.psum(1, "dp") * sum(g.size for g in gradients))
        me = lax.axis_index("dp")
        own = [lax.dynamic_slice_in_dim(w, me * one.shape[1], one.shape[1], 1).astype(jnp.float32) for w, one in zip(weights, m, strict=True)]
        new = [adamw(w, m, v, g) for w, m, v, g in zip(own, m, v, gradients, strict=True)]
        whole = [lax.all_gather(one[0], "dp", axis=1, tiled=True) for one in new]
        return (*whole, *(one[1] for one in new), *(one[2] for one in new))

    all_of, cut = P(None, None, None), P(None, "dp", None)
    return jax.shard_map(
        step,
        mesh=mesh,
        in_specs=(P(("rep", "dp"), None, None, None),) * 3 + (all_of,) * 3 + (cut,) * 6,
        out_specs=(P("rep", None, None),) * 3 + (P("rep", "dp", None),) * 6,
        check_vma=False,
    )
```

profile of v0, /device:TPU:21, one launch (start us, length us, event | category | flops | bytes accessed | tf_op | source)
XLA Modules:
  0.0 503.7 jit_solution(4829165397595578093)
XLA Ops:
  7.2 0.1 reduce-scatter.10.cloned.1.call-start
  7.3 39.1 %copy.21 = bf16[2,896,2560]{2,0,1:T(2,128)(2,1)} copy(bf16[2,896,2560]{2,1,0:T(8,128)(2,1)} %bitcast.15) | data formatting | bytes 18350080
  46.4 9.6 %copy.25 = bf16[112,8,2,2560]{3,1,2,0:T(8,128)(2,1)} copy(bf16[112,8,2,2560]{3,2,1,0:T(2,128)(2,1)} %bitcast.13) | data formatting | bytes 18350080
  56.0 0.1 reduce-scatter.10.cloned.1.call-update
  56.0 0.1 reduce-scatter.12.cloned.1.call-start
  56.1 39.1 %copy.23 = bf16[2,896,2560]{2,0,1:T(2,128)(2,1)} copy(bf16[2,896,2560]{2,1,0:T(8,128)(2,1)} %bitcast.16) | data formatting | bytes 18350080
  95.2 9.6 %copy.26 = bf16[112,8,2,2560]{3,1,2,0:T(8,128)(2,1)} copy(bf16[112,8,2,2560]{3,2,1,0:T(2,128)(2,1)} %bitcast.14) | data formatting | bytes 18350080
  104.8 0.1 reduce-scatter.12.cloned.1.call-update
  104.9 0.1 reduce-scatter.8.cloned.1.call-start
  104.9 0.7 reduce-scatter.8.cloned.1.call-update
  105.7 0.1 all-gather.8.cloned.1.call-start
  105.7 21.4 %reduce-scatter.10.cloned.1.call-done = bf16[56,5120]{1,0:T(8,128)(2,1)} async-done(((bf16[896,5120]{1,0:T(8,128)(2,1)}), bf16[56,5120]{1,0:T(8,128)(2,1)}) %reduce-scatter.10.cloned.1.call-update) | async-done | bytes 573456
  127.1 1.5 reshape.19
  128.6 69.4 %reduce-scatter.12.cloned.1.call-done = bf16[56,5120]{1,0:T(8,128)(2,1)} async-done(((bf16[896,5120]{1,0:T(8,128)(2,1)}), bf16[56,5120]{1,0:T(8,128)(2,1)}) %reduce-scatter.12.cloned.1.call-update) | async-done | bytes 573456
  198.0 1.6 reshape.21
  199.6 0.9 fusion.9
  201.8 66.5 %reduce-scatter.8.cloned.1.call-done = bf16[2,160,896]{2,1,0:T(8,128)(2,1)} async-done(((bf16[2,2560,896]{2,1,0:T(8,128)(2,1)}), bf16[2,160,896]{2,1,0:T(8,128)(2,1)}) %reduce-scatter.8.cloned.1.call-update) | async-done | bytes 573456 | tf_op jit(solution)/shard_map/reduce_scatter | solution.py:22
  268.3 2.0 fusion.11
  270.9 26.9 %psum.7 = f32[]{:T(128)} all-reduce(f32[]{:T(128)S(6)} %add.65), channel_id=1, replica_groups=mesh['rep'=4,'dp'=16] {'dp'}, use_global_device_ids=true, to_apply=%region_6.0 | all-reduce | flops 1 | bytes 8 | tf_op jit(solution)/shard_map/psum | solution.py:23
  298.6 3.1 fusion.17
  301.7 0.1 all-gather.8.cloned.1.call-update
  301.8 0.2 all-gather.4.cloned.1.call-start
  302.0 3.8 fusion.8
  305.8 0.1 all-gather.4.cloned.1.call-update
  305.9 0.1 all-gather.6.cloned.1.call-start
  306.0 2.9 fusion.14
  309.0 50.4 %all-gather.8.cloned.1.call-done = bf16[2,2560,896]{2,1,0:T(8,128)(2,1)} async-done(((bf16[2,160,896]{2,1,0:T(8,128)(2,1)}), bf16[2,2560,896]{2,1,0:T(8,128)(2,1)}) %all-gather.8.cloned.1.call-update) | async-done | bytes 9175056 | tf_op jit(solution)/shard_map/all_gather | solution.py:28
  359.4 56.8 %all-gather.4.cloned.1.call-done = bf16[2,896,2560]{2,1,0:T(8,128)(2,1)} async-done(((bf16[2,56,2560]{2,1,0:T(8,128)(2,1)}), bf16[2,896,2560]{2,1,0:T(8,128)(2,1)}) %all-gather.4.cloned.1.call-update) | async-done | bytes 9175056 | tf_op jit(solution)/shard_map/all_gather | solution.py:28
  416.3 56.8 %all-gather.6.cloned.1.call-done = bf16[2,896,2560]{2,1,0:T(8,128)(2,1)} async-done(((bf16[2,56,2560]{2,1,0:T(8,128)(2,1)}), bf16[2,896,2560]{2,1,0:T(8,128)(2,1)}) %all-gather.6.cloned.1.call-update) | async-done | bytes 9175056 | tf_op jit(solution)/shard_map/all_gather | solution.py:28
  473.1 7.8 %copy.40 = bf16[2,896,2560]{2,1,0:T(8,128)(2,1)} copy(bf16[2,896,2560]{2,1,0:T(8,128)(2,1)} %all-gather.4.cloned.1.call-done) | data formatting | bytes 18350080
  481.0 7.9 %copy.41 = bf16[2,896,2560]{2,1,0:T(8,128)(2,1)} copy(bf16[2,896,2560]{2,1,0:T(8,128)(2,1)} %all-gather.6.cloned.1.call-done) | data formatting | bytes 18350080
  488.8 8.0 %copy.42 = bf16[2,2560,896]{2,1,0:T(8,128)(2,1)} copy(bf16[2,2560,896]{2,1,0:T(8,128)(2,1)} %all-gather.8.cloned.1.call-done) | data formatting | bytes 18350080
  (9 shorter events, 0.1 us)
Async XLA Ops:
  7.2 119.9 %reduce-scatter.10.cloned.1.call-start = ((), (), s32[]{:S(2)}) async-start(), calls=%async_computation.7 | async-start | bytes 9748480
  56.0 142.0 %reduce-scatter.12.cloned.1.call-start = ((), (), s32[]{:S(2)}) async-start(), calls=%async_computation.8 | async-start | bytes 9748480
  104.9 163.5 %reduce-scatter.8.cloned.1.call-start = ((), (), s32[]{:S(2)}) async-start(), calls=%async_computation.3 | async-start | bytes 9748480 | tf_op jit(solution)/shard_map/reduce_scatter | solution.py:22
  105.7 253.8 %all-gather.8.cloned.1.call-start = ((), (), s32[]{:S(2)}) async-start(), calls=%async_computation.6 | async-start | bytes 9748480 | tf_op jit(solution)/shard_map/all_gather | solution.py:28
  198.0 100.6 %copy-start.1 = (f32[2,160,896]{2,1,0:T(8,128)S(1)}, f32[2,160,896]{2,1,0:T(8,128)}, u32[]{:S(2)}) copy-start(f32[2,160,896]{2,1,0:T(8,128)} %param.20) | copy-start | bytes 3440644
  199.6 99.0 %copy-start = (f32[2,160,896]{2,1,0:T(8,128)S(1)}, f32[2,160,896]{2,1,0:T(8,128)}, u32[]{:S(2)}) copy-start(f32[2,160,896]{2,1,0:T(8,128)} %param.23) | copy-start | bytes 3440644
  301.8 114.5 %all-gather.4.cloned.1.call-start = ((), (), s32[]{:S(2)}) async-start(), calls=%async_computation.4 | async-start | bytes 9748480 | tf_op jit(solution)/shard_map/all_gather | solution.py:28
  302.0 4.0 copy-start.2
  302.0 4.0 copy-start.3
  305.9 167.2 %all-gather.6.cloned.1.call-start = ((), (), s32[]{:S(2)}) async-start(), calls=%async_computation.5 | async-start | bytes 9748480 | tf_op jit(solution)/shard_map/all_gather | solution.py:28
Sparse Core Ops, SparseCore 0:
  56.1 70.9 reduce-scatter.9
  130.0 67.8 reduce-scatter.11
  200.4 67.9 reduce-scatter.7
  301.9 57.5 all-gather.7
  361.5 54.7 all-gather.3
  418.3 54.7 all-gather.5
where the time goes:
time: 504 us
  waiting for transfers between devices  322 us (64%)
  local copies, waits for them, and re-layouts  124 us (25%)
  blocking collectives  26.9 us (5%)
  between operations  16.9 us (3%)
  other arithmetic  12.8 us (3%)
    all_gather x3, waiting for transfers between devices, step(): whole = [lax.all_gather(one[0], 'dp', axis=1, tiled=True) for one in new]  164 us
    unnamed x17, local copies, waits for them, and re-layouts  124 us
    unnamed x8, waiting for transfers between devices  91.8 us
    reduce_scatter x1, waiting for transfers between devices, step(): lax.psum_scatter(t[0], 'dp', scatter_dimension=1, tiled=True)  66.5 us
    psum x1, blocking collectives, step(): squares = lax.psum(sum((jnp.sum(g * g) for g in gradients)), 'dp')  26.9 us
  transfers between devices with their start and end apart: 6, of which 6 were waited for; matrix products, arithmetic and copies ran while one was open for 12% of the time, Pallas kernels for 0%

commit v1 on v0

v1 whole, which is shorter than its diff:
```python
import functools
import math

import jax
import jax.numpy as jnp
from jax import lax
from jax.experimental import pallas as pl
from jax.experimental.pallas import tpu as pltpu
from jax.sharding import PartitionSpec as P

MESH = pl.DeviceIdType.MESH
F32, BF16 = jnp.float32, jnp.bfloat16


def row_tile(rows, columns):
    best = 8
    for tile in range(8, rows + 1, 8):
        if rows % tile == 0 and tile * columns <= 32 * 1024:
            best = tile
    return best


def kernel(n, count, *refs):
    g, w, m_in, v_in = (refs[i : i + 3] for i in range(0, 12, 3))
    layers, chips = g[0].shape[0], n // 2
    new = [refs[12 + k * layers : 12 + (k + 1) * layers] for k in range(3)]
    refs = refs[12 + 3 * layers :]
    m, v, own, held = (refs[i : i + 3] for i in range(0, 12, 3))
    (squares, own_sem, pair_send, pair_recv, ring_send, ring_recv, gather_recv, hand_send, hand_recv, norm_send, norm_recv, moment_sem, old_sem) = refs[12:]
    pieces = [(k, l) for k in range(3) for l in range(layers)]
    number = {piece: i for i, piece in enumerate(pieces)}
    me = lax.axis_index("dp")
    h, z = lax.rem(me, 2), lax.div(me, 2)
    partner = me + 1 - 2 * h
    onward = [lax.rem(me + 2, n), lax.rem(me + n - 2, n)]

    def remote(src, dst, send, recv, device):
        return pltpu.make_async_remote_copy(
            src_ref=src, dst_ref=dst, send_sem=send, recv_sem=recv, device_id={"dp": device}, device_id_type=MESH
        )

    def chunk(l, stage):
        return lax.rem(z + 2 * chips - 1 - stage, chips) if l == 0 else lax.rem(z + 1 + stage, chips)

    def own_copy(k, l, stage, slot):
        c = chunk(l, stage)
        return pltpu.make_async_copy(g[k].at[l, 2 * c + h], own[k].at[l, c], own_sem.at[slot, number[k, l]])

    def pair_copy(k, l, stage, slot):
        c = chunk(l, stage)
        i = number[k, l]
        return remote(g[k].at[l, 2 * c + 1 - h], new[k][l].at[2 * c + h], pair_send.at[slot, i], pair_recv.at[stage, i], partner)

    def ring_copy(k, l, stage):
        c = chunk(l, stage)
        i = number[k, l]
        return remote(own[k].at[l, c], new[k][l].at[2 * c + h], ring_send.at[i], ring_recv.at[stage, i], onward[l])

    def source(l, step):
        return lax.rem(z + 2 * chips - 1 - step, chips) if l == 0 else lax.rem(z + 1 + step, chips)

    def gather_copy(k, l, c, step):
        rows = new[k][l].at[2 * c + h]
        i = number[k, l]
        return remote(rows, rows, ring_send.at[i], gather_recv.at[step, i], onward[l])

    def hand_copy(k, l, c, step):
        rows = new[k][l].at[2 * c + h]
        i = number[k, l]
        return remote(rows, rows, hand_send.at[i], hand_recv.at[step, i], partner)

    for k, l in pieces:
        own_copy(k, l, 0, 0).start()

    barrier = pltpu.get_barrier_semaphore()

    def greet(j, _):
        pl.semaphore_signal(barrier, inc=1, device_id={"dp": lax.rem(me + j, n)}, device_id_type=MESH)
        return 0

    lax.fori_loop(1, n, greet, 0)
    pl.semaphore_wait(barrier, n - 1)

    for stage in range(2):
        for k, l in pieces:
            pair_copy(k, l, stage, stage).start()
            if stage:
                own_copy(k, l, stage, stage).start()

    def add(k, l, stage, arrived, total=0, squared=False):
        c = chunk(l, stage)
        rows, columns = own[k].shape[2:]
        tile = row_tile(rows, columns)

        def body(i, total):
            at = pl.ds(pl.multiple_of(i * tile, tile), tile)
            x = own[k][l, c, at, :].astype(F32) + new[k][l][2 * c + 1 - h, at, :].astype(F32)
            if arrived:
                x = x + new[k][l][2 * c + h, at, :].astype(F32)
            x = x.astype(BF16)
            own[k][l, c, at, :] = x
            if not squared:
                return total
            y = x.astype(F32)
            y = y * y
            y = sum(y[:, j : j + 128] for j in range(0, columns, 128))
            return total + sum(y[j : j + 8] for j in range(0, tile, 8))

        return lax.fori_loop(0, rows // tile, body, total)

    for k, l in pieces:
        own_copy(k, l, 0, 0).wait()
        pair_copy(k, l, 0, 0).wait_recv()
        add(k, l, 0, False)
        ring_copy(k, l, 0).start()
    for k, l in pieces:
        own_copy(k, l, 2, 0).start()
        pair_copy(k, l, 0, 0).wait_send()
        pair_copy(k, l, 2, 0).start()

    def middle(stage, _):
        slot = lax.rem(stage, 2)
        for k, l in pieces:
            own_copy(k, l, stage, slot).wait()
            pair_copy(k, l, stage, slot).wait_recv()
            ring_copy(k, l, stage - 1).wait_recv()
            add(k, l, stage, True)
            ring_copy(k, l, stage - 1).wait_send()
            ring_copy(k, l, stage).start()

            @pl.when(stage + 2 < chips)
            def _():
                own_copy(k, l, stage + 2, slot).start()
                pair_copy(k, l, stage, slot).wait_send()
                pair_copy(k, l, stage + 2, slot).start()

        return 0

    lax.fori_loop(1, chips - 2, middle, 0)

    for k, l in pieces:
        i = number[k, l]
        pltpu.make_async_copy(m_in[k].at[l], m[k].at[l], moment_sem.at[0, i]).start()
        pltpu.make_async_copy(v_in[k].at[l], v[k].at[l], moment_sem.at[1, i]).start()
        pltpu.make_async_copy(w[k].at[l, me], held[k].at[l], old_sem.at[i]).start()

    lax.fori_loop(chips - 2, chips - 1, middle, 0)

    last = chips - 1
    total = jnp.zeros((8, 128), F32)
    for k, l in pieces:
        own_copy(k, l, last, last % 2).wait()
        pair_copy(k, l, last, last % 2).wait_recv()
        ring_copy(k, l, last - 1).wait_recv()
        total = add(k, l, last, True, total, True)

    squares[me] = jnp.sum(total, axis=0, keepdims=True)

    def tell(j):
        return remote(squares.at[me], squares.at[me], norm_send.at[j], norm_recv.at[j], lax.rem(me + j, n))

    def tell_start(j, _):
        tell(j).start()
        return 0

    def tell_wait(j, _):
        tell(j).wait()
        return 0

    lax.fori_loop(1, n, tell_start, 0)
    for k, l in pieces:
        i = number[k, l]
        pltpu.make_async_copy(m_in[k].at[l], m[k].at[l], moment_sem.at[0, i]).wait()
        pltpu.make_async_copy(v_in[k].at[l], v[k].at[l], moment_sem.at[1, i]).wait()
        pltpu.make_async_copy(w[k].at[l, me], held[k].at[l], old_sem.at[i]).wait()
        ring_copy(k, l, last - 1).wait_send()
        for stage in (last - 1, last):
            pair_copy(k, l, stage, stage % 2).wait_send()
    lax.fori_loop(1, n, tell_wait, 0)
    everything = jnp.sum(squares[...], axis=0)
    everything = jnp.sum(everything, axis=1, keepdims=True)
    factor = jnp.minimum(1.0, 0.5 * lax.rsqrt(everything / count + 1e-30))

    for k, l in pieces:
        rows, columns = held[k].shape[1:]
        tile = row_tile(rows, columns)

        def body(i, _):
            at = pl.ds(pl.multiple_of(i * tile, tile), tile)
            x = own[k][l, z, at, :].astype(F32) * factor
            m_new = 0.9 * m[k][l, at, :] + 0.1 * x
            v_new = 0.95 * v[k][l, at, :] + 0.05 * x * x
            old = held[k][l, at, :].astype(F32)
            m[k][l, at, :] = m_new
            v[k][l, at, :] = v_new
            new[k][l][me, at, :] = (old - 0.02 * (m_new * lax.rsqrt(v_new + 1e-8) + 0.1 * old)).astype(BF16)
            return 0

        lax.fori_loop(0, rows // tile, body, 0)
        gather_copy(k, l, z, 0).start()
        hand_copy(k, l, z, 0).start()

    def forward(step, _):
        for k, l in pieces:
            c = source(l, step)
            gather_copy(k, l, c, step).wait_recv()
            gather_copy(k, l, c, step).wait_send()
            gather_copy(k, l, c, step + 1).start()
            hand_copy(k, l, c, step).wait_send()
            hand_copy(k, l, c, step + 1).start()
        return 0

    lax.fori_loop(0, chips - 2, forward, 0)
    for k, l in pieces:
        step = chips - 2
        c = source(l, step)
        gather_copy(k, l, c, step).wait_recv()
        gather_copy(k, l, c, step).wait_send()
        hand_copy(k, l, c, step).wait_send()
        hand_copy(k, l, c, step + 1).start()

    def handed(step, _):
        for k, l in pieces:
            hand_copy(k, l, z, step).wait_recv()
        return 0

    lax.fori_loop(0, chips, handed, 0)
    for k, l in pieces:
        hand_copy(k, l, z, chips - 1).wait_send()


def put_out(layers, *refs):
    new, moments = refs[: 3 * layers], refs[3 * layers : 3 * layers + 6]
    outs, sem = refs[3 * layers + 6 : -1], refs[-1]
    pairs = [(one, outs[i // layers].at[i % layers]) for i, one in enumerate(new)] + list(zip(moments, outs[3:]))
    copies = [pltpu.make_async_copy(one, out, sem.at[i]) for i, (one, out) in enumerate(pairs)]
    for copy in copies:
        copy.start()
    for copy in copies:
        copy.wait()


def solution(mesh):
    n = mesh.shape["dp"]

    def step(*arrays):
        terms, weights, m, v = (arrays[i : i + 3] for i in (0, 3, 6, 9))
        layers = m[0].shape[0]
        parts = [one.shape[1:] for one in m]
        count = float(n * layers * sum(math.prod(part) for part in parts))
        cut = lambda a, part: a.reshape(layers, n, *part)
        terms = [cut(t, part) for t, part in zip(terms, parts)]
        weights = [cut(t, part) for t, part in zip(weights, parts)]
        chips, pieces = n // 2, 3 * layers
        sem = pltpu.SemaphoreType.DMA
        outs = [pltpu.VMEM((n, *part), BF16) for part in parts for _ in range(layers)] + [pltpu.VMEM((layers, *part), F32) for part in parts] * 2
        result = pl.pallas_call(
            functools.partial(kernel, n, count),
            out_shape=outs,
            in_specs=[pl.BlockSpec(memory_space=pltpu.HBM)] * 12,
            out_specs=[pl.BlockSpec(memory_space=pltpu.VMEM)] * len(outs),
            scratch_shapes=[pltpu.VMEM((layers, chips, *part), BF16) for part in parts]
            + [pltpu.VMEM((layers, *part), BF16) for part in parts]
            + [
                pltpu.VMEM((n, 1, 128), F32),
                sem((2, pieces)),
                sem((2, pieces)),
                sem((chips, pieces)),
                sem((pieces,)),
                sem((chips - 1, pieces)),
                sem((chips - 1, pieces)),
                sem((pieces,)),
                sem((chips, pieces)),
                sem((n,)),
                sem((n,)),
                sem((2, pieces)),
                sem((pieces,)),
            ],
            compiler_params=pltpu.CompilerParams(collective_id=0, has_side_effects=True, vmem_limit_bytes=24 * 1024 * 1024),
        )(*(pltpu.with_memory_space_constraint(one, pltpu.HBM) for one in (*terms, *weights, *m, *v)))
        result = [pltpu.with_memory_space_constraint(one, pltpu.VMEM) for one in result]
        result = pl.pallas_call(
            functools.partial(put_out, layers),
            out_shape=[pltpu.HBM((layers, n, *part), BF16) for part in parts] + [pltpu.HBM((layers, *part), F32) for part in parts] * 2,
            in_specs=[pl.BlockSpec(memory_space=pltpu.VMEM)] * len(result),
            out_specs=[pl.BlockSpec(memory_space=pltpu.HBM)] * 9,
            scratch_shapes=[sem((len(result),))],
            compiler_params=pltpu.CompilerParams(vmem_limit_bytes=1024 * 1024),
        )(*result)
        whole = [one.reshape(layers, -1, one.shape[-1]) for one in result[:3]]
        return (*whole, *result[3:])

    all_of, cut = P(None, None, None), P(None, "dp", None)
    return jax.shard_map(
        step,
        mesh=mesh,
        in_specs=(P(("rep", "dp"), None, None, None),) * 3 + (all_of,) * 3 + (cut,) * 6,
        out_specs=(P("rep", None, None),) * 3 + (P("rep", "dp", None),) * 6,
        check_vma=False,
    )
```

time: 504 us -> 305 us (0.61)
  waiting for transfers between devices: 322 us -> 0 us
  Pallas kernels: 0 us -> 295 us
  local copies, waits for them, and re-layouts: 124 us -> 8.88 us
  blocking collectives: 26.9 us -> 0 us
  between operations: 16.9 us -> 0.67 us
  other arithmetic: 12.8 us -> 0 us
    pallas_call x0 -> x2, Pallas kernels: none -> 295 us  [the longest x1 284 us: step(): pl.pallas_call(functools.partial(kernel, n, count), out_shape=outs, in_sp...]
    all_gather x3 -> x0, waiting for transfers between devices: 164 us -> none  [step(): whole = [lax.all_gather(one[0], 'dp', axis=1, tiled=True) for one in new]]
    unnamed x17 -> x8, local copies, waits for them, and re-layouts: 124 us -> 8.88 us
    unnamed x8 -> x0, waiting for transfers between devices: 91.8 us -> none
    reduce_scatter x1 -> x0, waiting for transfers between devices: 66.5 us -> none  [step(): lax.psum_scatter(t[0], 'dp', scatter_dimension=1, tiled=True)]
    psum x1 -> x0, blocking collectives: 26.9 us -> none  [step(): squares = lax.psum(sum((jnp.sum(g * g) for g in gradients)), 'dp')]
    convert_element_type x3 -> x0, other arithmetic: 9.88 us -> none  [adamw(): return ((w - 0.02 * step).astype(jnp.bfloat16), m, v)]
  transfers between devices with their start and end apart: 6 -> 0, of which waited for: 6 -> 0; matrix products, arithmetic and copies ran while one was open for 12% -> 0% of each run, Pallas kernels for 0% -> 0%
where the time goes in v1:
time: 305 us; the launch traced here: 304 us
  Pallas kernels  295 us (97%)
  local copies, waits for them, and re-layouts  8.88 us (3%)
    pallas_call x1, Pallas kernels, step(): pl.pallas_call(functools.partial(kernel, n, count), out_shape=outs, in_sp...  284 us
    pallas_call x1, Pallas kernels, step(): pl.pallas_call(functools.partial(put_out, layers), out_shape=[pltpu.HBM((...  11.2 us
    unnamed x8, local copies, waits for them, and re-layouts  8.88 us

profile of v1, /device:TPU:21, one launch (start us, length us, event | category | flops | bytes accessed | tf_op | source)
XLA Modules:
  0.0 304.4 jit_solution(6899443319356397814)
XLA Ops:
  0.6 283.7 %shard_map.187 = (bf16[16,56,2560]{2,1,0:T(8,128)(2,1)S(1)}, bf16[16,56,2560]{2,1,0:T(8,128)(2,1)S(1)}, bf16[16,56,2560]{2,1,0:T(8,128)(2,1)S(1)}, bf16[16,56,25...) custom-call(bf16[2,16,56,2560]{3,2,1,0:T(8,128)(2,1)} %bitcast.9, ...), custom_call_target="tpu_custom_call" | custom-call | tf_op jit(solution)/shard_map/pallas_call | solution.py:257
  284.3 0.0 copy-start
  284.3 2.1 copy-done
  286.5 0.0 copy-start.2
  286.5 2.1 copy-done.2
  288.6 0.0 copy-start.1
  288.6 2.3 copy-done.1
  290.9 0.0 copy-start.3
  290.9 2.3 copy-done.3
  293.2 11.2 %shard_map.188 = (bf16[2,16,56,2560]{3,2,1,0:T(8,128)(2,1)}, bf16[2,16,56,2560]{3,2,1,0:T(8,128)(2,1)}, bf16[2,16,160,896]{3,2,1,0:T(8,128)(2,1)}, f32[2,56,2560...) custom-call(bf16[16,56,2560]{2,1,0:T(8,128)(2,1)S(1)} %get-tuple-ele, ...), custom_call_target="tpu_custom_call" | custom-call | tf_op jit(solution)/shard_map/pallas_call | solution.py:282
Async XLA Ops:
  284.3 2.1 copy-start
  286.5 2.1 copy-start.2
  288.6 2.3 copy-start.1
  290.9 2.3 copy-start.3

commit v2 on v1

--- a/solution.py
+++ b/solution.py
@@ -285,7 +285,7 @@
             in_specs=[pl.BlockSpec(memory_space=pltpu.VMEM)] * len(result),
             out_specs=[pl.BlockSpec(memory_space=pltpu.HBM)] * 9,
             scratch_shapes=[sem((len(result),))],
-            compiler_params=pltpu.CompilerParams(vmem_limit_bytes=1024 * 1024),
+            compiler_params=pltpu.CompilerParams(vmem_limit_bytes=24 * 1024 * 1024),
         )(*result)
         whole = [one.reshape(layers, -1, one.shape[-1]) for one in result[:3]]
         return (*whole, *result[3:])

time: 305 us -> 296 us (0.970)
  local copies, waits for them, and re-layouts: 8.88 us -> 0 us
    unnamed x8 -> x0, local copies, waits for them, and re-layouts: 8.88 us -> none
where the time goes in v2:
time: 296 us
  Pallas kernels  295 us (100%)
    pallas_call x1, Pallas kernels, step(): pl.pallas_call(functools.partial(kernel, n, count), out_shape=outs, in_sp...  284 us
    pallas_call x1, Pallas kernels, step(): pl.pallas_call(functools.partial(put_out, layers), out_shape=[pltpu.HBM((...  11.3 us

profile of v2, /device:TPU:21, one launch (start us, length us, event | category | flops | bytes accessed | tf_op | source)
XLA Modules:
  0.0 295.6 jit_solution(3241955879952223279)
XLA Ops:
  0.6 283.7 %shard_map.187 = (bf16[16,56,2560]{2,1,0:T(8,128)(2,1)S(1)}, bf16[16,56,2560]{2,1,0:T(8,128)(2,1)S(1)}, bf16[16,56,2560]{2,1,0:T(8,128)(2,1)S(1)}, bf16[16,56,25...) custom-call(bf16[2,16,56,2560]{3,2,1,0:T(8,128)(2,1)} %bitcast.9, ...), custom_call_target="tpu_custom_call" | custom-call | tf_op jit(solution)/shard_map/pallas_call | solution.py:257
  284.3 11.3 %shard_map.188 = (bf16[2,16,56,2560]{3,2,1,0:T(8,128)(2,1)}, bf16[2,16,56,2560]{3,2,1,0:T(8,128)(2,1)}, bf16[2,16,160,896]{3,2,1,0:T(8,128)(2,1)}, f32[2,56,2560...) custom-call(bf16[16,56,2560]{2,1,0:T(8,128)(2,1)S(1)} %get-tuple-ele, ...), custom_call_target="tpu_custom_call" | custom-call | tf_op jit(solution)/shard_map/pallas_call | solution.py:282

commit v3 on v0

v3 whole, which is shorter than its diff:
```python
import functools
import math

import jax
import jax.numpy as jnp
from jax import lax
from jax.experimental import pallas as pl
from jax.experimental.pallas import tpu as pltpu
from jax.sharding import PartitionSpec as P

MESH = pl.DeviceIdType.MESH
F32, BF16 = jnp.float32, jnp.bfloat16


def row_tile(rows, columns):
    best = 8
    for tile in range(8, rows + 1, 8):
        if rows % tile == 0 and tile * columns <= 32 * 1024:
            best = tile
    return best


def cuts(parts):
    *most, (rows, _) = parts
    small = rows // 5 // 8 * 8
    k = len(most)
    return [(k, 0, small), *((i, 0, part[0]) for i, part in enumerate(most)), (k, small, rows - 2 * small), (k, rows - small, small)]


def kernel(n, count, *refs):
    g, w, m_in, v_in = (refs[i : i + 3] for i in range(0, 12, 3))
    layers, chips = g[0].shape[0], n // 2
    new = [refs[12 + k * layers : 12 + (k + 1) * layers] for k in range(3)]
    refs = refs[12 + 3 * layers :]
    m, v, own, held = (refs[i : i + 3] for i in range(0, 12, 3))
    (squares, own_sem, pair_send, pair_recv, ring_send, ring_recv, hand_send, norm_send, norm_recv, state_sem, held_sem) = refs[12:]
    pieces = [(k, l, first, rows) for k, first, rows in cuts([one.shape[1:] for one in held]) for l in range(layers)]
    blocks = [(k, l) for k in range(3) for l in range(layers)]
    me = lax.axis_index("dp")
    h, z = lax.rem(me, 2), lax.div(me, 2)
    partner = me + 1 - 2 * h
    up, down = lax.rem(me + 2, n), lax.rem(me + n - 2, n)
    onward = [up, down]

    def remote(src, dst, send, recv, device):
        return pltpu.make_async_remote_copy(
            src_ref=src, dst_ref=dst, send_sem=send, recv_sem=recv, device_id={"dp": device}, device_id_type=MESH
        )

    def chunk(l, stage):
        return lax.rem(z + 2 * chips - 1 - stage, chips) if l == 0 else lax.rem(z + 1 + stage, chips)

    def own_copy(i, stage):
        k, l, first, rows = pieces[i]
        c, at = chunk(l, stage), pl.ds(first, rows)
        return pltpu.make_async_copy(g[k].at[l, 2 * c + h, at], own[k].at[l, c, at], own_sem.at[i])

    def held_copy(k, l):
        return pltpu.make_async_copy(g[k].at[l, 2 * chunk(l, 0) + 1 - h], held[k].at[l], held_sem.at[k, l])

    def pair_copy(i, stage, start=False):
        k, l, first, rows = pieces[i]
        c, at = chunk(l, stage), pl.ds(first, rows)
        src = held[k].at[l, at] if start else g[k].at[l, 2 * c + 1 - h, at]
        return remote(src, new[k][l].at[2 * c + h, at], pair_send.at[i], pair_recv.at[stage, i], partner)

    def ring_copy(i, stage):
        k, l, first, rows = pieces[i]
        c, at = chunk(l, stage), pl.ds(first, rows)
        return remote(own[k].at[l, c, at], new[k][l].at[2 * c + h, at], ring_send.at[i], ring_recv.at[stage, i], onward[l])

    def gather_copy(i, c, step):
        k, l, first, rows = pieces[i]
        block = new[k][l].at[2 * c + h, pl.ds(first, rows)]
        return remote(block, block, ring_send.at[i], ring_recv.at[step, i], onward[l])

    def hand_copy(i, c, step):
        k, l, first, rows = pieces[i]
        block = new[k][l].at[2 * c + h, pl.ds(first, rows)]
        return remote(block, block, hand_send.at[i], pair_recv.at[step, i], partner)

    def state_copies(k, l):
        return [
            pltpu.make_async_copy(m_in[k].at[l], m[k].at[l], state_sem.at[0, k, l]),
            pltpu.make_async_copy(v_in[k].at[l], v[k].at[l], state_sem.at[1, k, l]),
            pltpu.make_async_copy(w[k].at[l, me], held[k].at[l], held_sem.at[k, l]),
        ]

    def add(i, stage, arrived, total=0, squared=False):
        k, l, first, rows = pieces[i]
        c = chunk(l, stage)
        columns = own[k].shape[-1]
        tile = row_tile(rows, columns)

        def body(j, total):
            at = pl.ds(pl.multiple_of(first + j * tile, 8), tile)
            x = own[k][l, c, at, :].astype(F32) + new[k][l][2 * c + 1 - h, at, :].astype(F32)
            if arrived:
                x = x + new[k][l][2 * c + h, at, :].astype(F32)
            x = x.astype(BF16)
            own[k][l, c, at, :] = x
            if not squared:
                return total
            y = x.astype(F32)
            y = y * y
            y = sum(y[:, j : j + 128] for j in range(0, columns, 128))
            return total + sum(y[j : j + 8] for j in range(0, tile, 8))

        return lax.fori_loop(0, rows // tile, body, total)

    everyone = range(len(pieces))

    for k, l in blocks:
        held_copy(k, l).start()
    for i in everyone:
        own_copy(i, 0).start()

    barrier = pltpu.get_barrier_semaphore()
    for other in (partner, up, down):
        pl.semaphore_signal(barrier, inc=1, device_id={"dp": other}, device_id_type=MESH)
    for k, l in blocks:
        held_copy(k, l).wait()
    pl.semaphore_wait(barrier, 3)

    for i in everyone:
        pair_copy(i, 0, True).start()
    for i in everyone:
        own_copy(i, 0).wait()
        pair_copy(i, 0).wait_recv()
        add(i, 0, False)
        ring_copy(i, 0).start()
    for i in everyone:
        pair_copy(i, 0).wait_send()
        own_copy(i, 1).start()
        pair_copy(i, 1).start()
    for k, l in blocks:
        for copy in state_copies(k, l):
            copy.start()

    def middle(stage, _):
        for i in everyone:
            own_copy(i, stage).wait()
            pair_copy(i, stage).wait_recv()
            ring_copy(i, stage - 1).wait_recv()
            add(i, stage, True)
            ring_copy(i, stage - 1).wait_send()
            ring_copy(i, stage).start()
            pair_copy(i, stage).wait_send()
            own_copy(i, stage + 1).start()
            pair_copy(i, stage + 1).start()
        return 0

    last = chips - 1
    lax.fori_loop(1, last, middle, 0)
    total = jnp.zeros((8, 128), F32)
    for i in everyone:
        own_copy(i, last).wait()
        pair_copy(i, last).wait_recv()
        ring_copy(i, last - 1).wait_recv()
        total = add(i, last, True, total, True)

    squares[me] = jnp.sum(total, axis=0, keepdims=True)
    far = sorted(range(1, n), key=lambda j: -min(j, n - j))
    tell = [remote(squares.at[me], squares.at[me], norm_send.at[j], norm_recv.at[j], lax.rem(me + j, n)) for j in far]
    for one in tell:
        one.start()
    for k, l in blocks:
        for copy in state_copies(k, l):
            copy.wait()
    for i in everyone:
        ring_copy(i, last - 1).wait_send()
        pair_copy(i, last).wait_send()
    for one in tell[::-1]:
        one.wait_recv()
    everything = jnp.sum(jnp.sum(squares[...], axis=0), axis=1, keepdims=True)
    factor = jnp.minimum(1.0, 0.5 * lax.rsqrt(everything / count + 1e-30))

    for i in everyone:
        k, l, first, rows = pieces[i]
        tile = row_tile(rows, held[k].shape[-1])

        def body(j, _):
            at = pl.ds(pl.multiple_of(first + j * tile, 8), tile)
            x = own[k][l, z, at, :].astype(F32) * factor
            m_new = 0.9 * m[k][l, at, :] + 0.1 * x
            v_new = 0.95 * v[k][l, at, :] + 0.05 * x * x
            old = held[k][l, at, :].astype(F32)
            m[k][l, at, :] = m_new
            v[k][l, at, :] = v_new
            new[k][l][me, at, :] = (old - 0.02 * (m_new * lax.rsqrt(v_new + 1e-8) + 0.1 * old)).astype(BF16)
            return 0

        lax.fori_loop(0, rows // tile, body, 0)
        gather_copy(i, z, 0).start()
        hand_copy(i, z, 0).start()

    def forward(step, _):
        for i in everyone:
            c = chunk(pieces[i][1], step)
            gather_copy(i, c, step).wait_recv()
            gather_copy(i, c, step).wait_send()
            gather_copy(i, c, step + 1).start()
            hand_copy(i, c, step).wait_send()
            hand_copy(i, c, step + 1).start()
        return 0

    lax.fori_loop(0, last - 1, forward, 0)
    for i in everyone:
        c = chunk(pieces[i][1], last - 1)
        gather_copy(i, c, last - 1).wait_recv()
        hand_copy(i, c, last - 1).wait_send()
        hand_copy(i, c, last).start()
    for i in everyone:
        gather_copy(i, z, last - 1).wait_send()
    for one in tell:
        one.wait_send()

    def handed(step, _):
        for i in everyone:
            hand_copy(i, z, step).wait_recv()
        return 0

    lax.fori_loop(0, chips, handed, 0)
    for i in everyone:
        hand_copy(i, z, last).wait_send()


def put_out(layers, *refs):
    new, moments = refs[: 3 * layers], refs[3 * layers : 3 * layers + 6]
    outs, sem = refs[3 * layers + 6 : -1], refs[-1]
    pairs = [(one, outs[i // layers].at[i % layers]) for i, one in enumerate(new)] + list(zip(moments, outs[3:]))
    copies = [pltpu.make_async_copy(one, out, sem.at[i]) for i, (one, out) in enumerate(pairs)]
    for copy in copies:
        copy.start()
    for copy in copies:
        copy.wait()


def solution(mesh):
    n = mesh.shape["dp"]

    def step(*arrays):
        terms, weights, m, v = (arrays[i : i + 3] for i in (0, 3, 6, 9))
        layers = m[0].shape[0]
        parts = [one.shape[1:] for one in m]
        count = float(n * layers * sum(math.prod(part) for part in parts))
        cut = lambda a, part: a.reshape(layers, n, *part)
        terms = [cut(t, part) for t, part in zip(terms, parts)]
        weights = [cut(t, part) for t, part in zip(weights, parts)]
        chips, pieces = n // 2, layers * len(cuts(parts))
        sem = pltpu.SemaphoreType.DMA
        outs = [pltpu.VMEM((n, *part), BF16) for part in parts for _ in range(layers)] + [pltpu.VMEM((layers, *part), F32) for part in parts] * 2
        grant = 24 * 1024 * 1024
        result = pl.pallas_call(
            functools.partial(kernel, n, count),
            out_shape=outs,
            in_specs=[pl.BlockSpec(memory_space=pltpu.HBM)] * 12,
            out_specs=[pl.BlockSpec(memory_space=pltpu.VMEM)] * len(outs),
            scratch_shapes=[pltpu.VMEM((layers, chips, *part), BF16) for part in parts]
            + [pltpu.VMEM((layers, *part), BF16) for part in parts]
            + [
                pltpu.VMEM((n, 1, 128), F32),
                sem((pieces,)),
                sem((pieces,)),
                sem((chips, pieces)),
                sem((pieces,)),
                sem((chips - 1, pieces)),
                sem((pieces,)),
                sem((n,)),
                sem((n,)),
                sem((2, 3, layers)),
                sem((3, layers)),
            ],
            compiler_params=pltpu.CompilerParams(collective_id=0, has_side_effects=True, vmem_limit_bytes=grant),
        )(*(pltpu.with_memory_space_constraint(one, pltpu.HBM) for one in (*terms, *weights, *m, *v)))
        result = [pltpu.with_memory_space_constraint(one, pltpu.VMEM) for one in result]
        result = pl.pallas_call(
            functools.partial(put_out, layers),
            out_shape=[pltpu.HBM((layers, n, *part), BF16) for part in parts] + [pltpu.HBM((layers, *part), F32) for part in parts] * 2,
            in_specs=[pl.BlockSpec(memory_space=pltpu.VMEM)] * len(result),
            out_specs=[pl.BlockSpec(memory_space=pltpu.HBM)] * 9,
            scratch_shapes=[sem((len(result),))],
            compiler_params=pltpu.CompilerParams(vmem_limit_bytes=grant),
        )(*result)
        whole = [one.reshape(layers, -1, one.shape[-1]) for one in result[:3]]
        return (*whole, *result[3:])

    all_of, cut = P(None, None, None), P(None, "dp", None)
    return jax.shard_map(
        step,
        mesh=mesh,
        in_specs=(P(("rep", "dp"), None, None, None),) * 3 + (all_of,) * 3 + (cut,) * 6,
        out_specs=(P("rep", None, None),) * 3 + (P("rep", "dp", None),) * 6,
        check_vma=False,
    )
```

time: 504 us -> 292 us (0.58)
  waiting for transfers between devices: 322 us -> 0 us
  Pallas kernels: 0 us -> 292 us
  local copies, waits for them, and re-layouts: 124 us -> 0 us
  blocking collectives: 26.9 us -> 0 us
  between operations: 16.9 us -> 0.66 us
  other arithmetic: 12.8 us -> 0 us
    pallas_call x0 -> x2, Pallas kernels: none -> 292 us  [the longest x1 280 us: step(): pl.pallas_call(functools.partial(kernel, n, count), out_shape=outs, in_sp...]
    all_gather x3 -> x0, waiting for transfers between devices: 164 us -> none  [step(): whole = [lax.all_gather(one[0], 'dp', axis=1, tiled=True) for one in new]]
    unnamed x17 -> x0, local copies, waits for them, and re-layouts: 124 us -> none
    unnamed x8 -> x0, waiting for transfers between devices: 91.8 us -> none
    reduce_scatter x1 -> x0, waiting for transfers between devices: 66.5 us -> none  [step(): lax.psum_scatter(t[0], 'dp', scatter_dimension=1, tiled=True)]
    psum x1 -> x0, blocking collectives: 26.9 us -> none  [step(): squares = lax.psum(sum((jnp.sum(g * g) for g in gradients)), 'dp')]
    convert_element_type x3 -> x0, other arithmetic: 9.88 us -> none  [adamw(): return ((w - 0.02 * step).astype(jnp.bfloat16), m, v)]
  transfers between devices with their start and end apart: 6 -> 0, of which waited for: 6 -> 0; matrix products, arithmetic and copies ran while one was open for 12% -> 0% of each run, Pallas kernels for 0% -> 0%
where the time goes in v3:
time: 292 us
  Pallas kernels  292 us (100%)
    pallas_call x1, Pallas kernels, step(): pl.pallas_call(functools.partial(kernel, n, count), out_shape=outs, in_sp...  280 us
    pallas_call x1, Pallas kernels, step(): pl.pallas_call(functools.partial(put_out, layers), out_shape=[pltpu.HBM((...  11.3 us

profile of v3, /device:TPU:21, one launch (start us, length us, event | category | flops | bytes accessed | tf_op | source)
XLA Modules:
  0.0 292.3 jit_solution(5855636788657330152)
XLA Ops:
  0.6 280.4 %shard_map.187 = (bf16[16,56,2560]{2,1,0:T(8,128)(2,1)S(1)}, bf16[16,56,2560]{2,1,0:T(8,128)(2,1)S(1)}, bf16[16,56,2560]{2,1,0:T(8,128)(2,1)S(1)}, bf16[16,56,25...) custom-call(bf16[2,16,56,2560]{3,2,1,0:T(8,128)(2,1)} %bitcast.9, ...), custom_call_target="tpu_custom_call" | custom-call | tf_op jit(solution)/shard_map/pallas_call | solution.py:254
  281.1 11.3 %shard_map.188 = (bf16[2,16,56,2560]{3,2,1,0:T(8,128)(2,1)}, bf16[2,16,56,2560]{3,2,1,0:T(8,128)(2,1)}, bf16[2,16,160,896]{3,2,1,0:T(8,128)(2,1)}, f32[2,56,2560...) custom-call(bf16[16,56,2560]{2,1,0:T(8,128)(2,1)S(1)} %get-tuple-ele, ...), custom_call_target="tpu_custom_call" | custom-call | tf_op jit(solution)/shard_map/pallas_call | solution.py:277

commit v4 on v3

--- a/solution.py
+++ b/solution.py
@@ -33,9 +33,9 @@
     new = [refs[12 + k * layers : 12 + (k + 1) * layers] for k in range(3)]
     refs = refs[12 + 3 * layers :]
     m, v, own, held = (refs[i : i + 3] for i in range(0, 12, 3))
-    (squares, own_sem, pair_send, pair_recv, ring_send, ring_recv, hand_send, norm_send, norm_recv, state_sem, held_sem) = refs[12:]
+    (squares, own_sem, held_sem, pair_send, pair_recv, ring_send, ring_recv, hand_send, hand_recv, norm_send, norm_recv) = refs[12:]
     pieces = [(k, l, first, rows) for k, first, rows in cuts([one.shape[1:] for one in held]) for l in range(layers)]
-    blocks = [(k, l) for k in range(3) for l in range(layers)]
+    weights = range(3)
     me = lax.axis_index("dp")
     h, z = lax.rem(me, 2), lax.div(me, 2)
     partner = me + 1 - 2 * h
@@ -55,36 +55,42 @@
         c, at = chunk(l, stage), pl.ds(first, rows)
         return pltpu.make_async_copy(g[k].at[l, 2 * c + h, at], own[k].at[l, c, at], own_sem.at[i])
 
-    def held_copy(k, l):
-        return pltpu.make_async_copy(g[k].at[l, 2 * chunk(l, 0) + 1 - h], held[k].at[l], held_sem.at[k, l])
+    def held_copy(i):
+        k, l, first, rows = pieces[i]
+        at = pl.ds(first, rows)
+        return pltpu.make_async_copy(g[k].at[l, 2 * chunk(l, 0) + 1 - h, at], held[k].at[l, at], held_sem.at[i])
 
     def pair_copy(i, stage, start=False):
         k, l, first, rows = pieces[i]
         c, at = chunk(l, stage), pl.ds(first, rows)
         src = held[k].at[l, at] if start else g[k].at[l, 2 * c + 1 - h, at]
-        return remote(src, new[k][l].at[2 * c + h, at], pair_send.at[i], pair_recv.at[stage, i], partner)
+        return remote(src, new[k][l].at[2 * c + h, at], pair_send.at[k], pair_recv.at[lax.rem(stage, 2), i], partner)
 
     def ring_copy(i, stage):
         k, l, first, rows = pieces[i]
         c, at = chunk(l, stage), pl.ds(first, rows)
-        return remote(own[k].at[l, c, at], new[k][l].at[2 * c + h, at], ring_send.at[i], ring_recv.at[stage, i], onward[l])
+        return remote(own[k].at[l, c, at], new[k][l].at[2 * c + h, at], ring_send.at[k], ring_recv.at[stage, i], onward[l])
 
     def gather_copy(i, c, step):
         k, l, first, rows = pieces[i]
         block = new[k][l].at[2 * c + h, pl.ds(first, rows)]
-        return remote(block, block, ring_send.at[i], ring_recv.at[step, i], onward[l])
-
-    def hand_copy(i, c, step):
+        return remote(block, block, ring_send.at[k], ring_recv.at[step, i], onward[l])
+
+    def hand_copy(i, c):
         k, l, first, rows = pieces[i]
         block = new[k][l].at[2 * c + h, pl.ds(first, rows)]
-        return remote(block, block, hand_send.at[i], pair_recv.at[step, i], partner)
-
-    def state_copies(k, l):
+        return remote(block, block, hand_send.at[k], hand_recv.at[k], partner)
+
+    def state_copies(k):
         return [
-            pltpu.make_async_copy(m_in[k].at[l], m[k].at[l], state_sem.at[0, k, l]),
-            pltpu.make_async_copy(v_in[k].at[l], v[k].at[l], state_sem.at[1, k, l]),
-            pltpu.make_async_copy(w[k].at[l, me], held[k].at[l], held_sem.at[k, l]),
+            pltpu.make_async_copy(m_in[k], m[k], held_sem.at[k]),
+            pltpu.make_async_copy(v_in[k], v[k], held_sem.at[3 + k]),
+            pltpu.make_async_copy(w[k].at[:, me], held[k], held_sem.at[6 + k]),
         ]
+
+    def all_of(k, stages, send, recv):
+        block = own[k].at[:, pl.ds(0, stages)]
+        return remote(block, block, send.at[k], recv.at[k], partner)
 
     def add(i, stage, arrived, total=0, squared=False):
         k, l, first, rows = pieces[i]
@@ -110,31 +116,30 @@
 
     everyone = range(len(pieces))
 
-    for k, l in blocks:
-        held_copy(k, l).start()
-    for i in everyone:
+    for i in everyone:
+        held_copy(i).start()
         own_copy(i, 0).start()
 
     barrier = pltpu.get_barrier_semaphore()
     for other in (partner, up, down):
         pl.semaphore_signal(barrier, inc=1, device_id={"dp": other}, device_id_type=MESH)
-    for k, l in blocks:
-        held_copy(k, l).wait()
     pl.semaphore_wait(barrier, 3)
 
     for i in everyone:
+        held_copy(i).wait()
         pair_copy(i, 0, True).start()
     for i in everyone:
         own_copy(i, 0).wait()
         pair_copy(i, 0).wait_recv()
         add(i, 0, False)
         ring_copy(i, 0).start()
-    for i in everyone:
-        pair_copy(i, 0).wait_send()
+    for k in weights:
+        all_of(k, 1, pair_send, hand_recv).wait_send()
+    for i in everyone:
         own_copy(i, 1).start()
         pair_copy(i, 1).start()
-    for k, l in blocks:
-        for copy in state_copies(k, l):
+    for k in weights:
+        for copy in state_copies(k):
             copy.start()
 
     def middle(stage, _):
@@ -143,9 +148,7 @@
             pair_copy(i, stage).wait_recv()
             ring_copy(i, stage - 1).wait_recv()
             add(i, stage, True)
-            ring_copy(i, stage - 1).wait_send()
             ring_copy(i, stage).start()
-            pair_copy(i, stage).wait_send()
             own_copy(i, stage + 1).start()
             pair_copy(i, stage + 1).start()
         return 0
@@ -161,17 +164,15 @@
 
     squares[me] = jnp.sum(total, axis=0, keepdims=True)
     far = sorted(range(1, n), key=lambda j: -min(j, n - j))
-    tell = [remote(squares.at[me], squares.at[me], norm_send.at[j], norm_recv.at[j], lax.rem(me + j, n)) for j in far]
-    for one in tell:
-        one.start()
-    for k, l in blocks:
-        for copy in state_copies(k, l):
+    for j in far:
+        remote(squares.at[me], squares.at[me], norm_send, norm_recv, lax.rem(me + j, n)).start()
+    for k in weights:
+        for copy in state_copies(k):
             copy.wait()
-    for i in everyone:
-        ring_copy(i, last - 1).wait_send()
-        pair_copy(i, last).wait_send()
-    for one in tell[::-1]:
-        one.wait_recv()
+        all_of(k, last, ring_send, hand_recv).wait_send()
+        all_of(k, last, pair_send, hand_recv).wait_send()
+    others = squares.at[pl.ds(0, n - 1)]
+    remote(others, others, norm_send, norm_recv, partner).wait_recv()
     everything = jnp.sum(jnp.sum(squares[...], axis=0), axis=1, keepdims=True)
     factor = jnp.minimum(1.0, 0.5 * lax.rsqrt(everything / count + 1e-30))
 
@@ -192,37 +193,26 @@
 
         lax.fori_loop(0, rows // tile, body, 0)
         gather_copy(i, z, 0).start()
-        hand_copy(i, z, 0).start()
+        hand_copy(i, z).start()
 
     def forward(step, _):
         for i in everyone:
             c = chunk(pieces[i][1], step)
             gather_copy(i, c, step).wait_recv()
-            gather_copy(i, c, step).wait_send()
             gather_copy(i, c, step + 1).start()
-            hand_copy(i, c, step).wait_send()
-            hand_copy(i, c, step + 1).start()
+            hand_copy(i, c).start()
         return 0
 
     lax.fori_loop(0, last - 1, forward, 0)
     for i in everyone:
         c = chunk(pieces[i][1], last - 1)
         gather_copy(i, c, last - 1).wait_recv()
-        hand_copy(i, c, last - 1).wait_send()
-        hand_copy(i, c, last).start()
-    for i in everyone:
-        gather_copy(i, z, last - 1).wait_send()
-    for one in tell:
-        one.wait_send()
-
-    def handed(step, _):
-        for i in everyone:
-            hand_copy(i, z, step).wait_recv()
-        return 0
-
-    lax.fori_loop(0, chips, handed, 0)
-    for i in everyone:
-        hand_copy(i, z, last).wait_send()
+        hand_copy(i, c).start()
+    remote(others, others, norm_send, norm_recv, partner).wait_send()
+    for k in weights:
+        all_of(k, last, ring_send, hand_recv).wait_send()
+    for k in weights:
+        all_of(k, chips, hand_send, hand_recv).wait()
 
 
 def put_out(layers, *refs):
@@ -262,14 +252,14 @@
                 pltpu.VMEM((n, 1, 128), F32),
                 sem((pieces,)),
                 sem((pieces,)),
-                sem((chips, pieces)),
-                sem((pieces,)),
+                sem((3,)),
+                sem((2, pieces)),
+                sem((3,)),
                 sem((chips - 1, pieces)),
-                sem((pieces,)),
-                sem((n,)),
-                sem((n,)),
-                sem((2, 3, layers)),
-                sem((3, layers)),
+                sem((3,)),
+                sem((3,)),
+                sem,
+                sem,
             ],
             compiler_params=pltpu.CompilerParams(collective_id=0, has_side_effects=True, vmem_limit_bytes=grant),
         )(*(pltpu.with_memory_space_constraint(one, pltpu.HBM) for one in (*terms, *weights, *m, *v)))

time: 292 us -> 291 us (level)
  no operation moved by 1% of the time
where the time goes in v4:
time: 291 us
  Pallas kernels  290 us (100%)
    pallas_call x1, Pallas kernels, step(): pl.pallas_call(functools.partial(kernel, n, count), out_shape=outs, in_sp...  279 us
    pallas_call x1, Pallas kernels, step(): pl.pallas_call(functools.partial(put_out, layers), out_shape=[pltpu.HBM((...  11.3 us

profile of v4, /device:TPU:21, one launch (start us, length us, event | category | flops | bytes accessed | tf_op | source)
XLA Modules:
  0.0 290.5 jit_solution(11112629875159403629)
XLA Ops:
  0.6 278.6 %shard_map.187 = (bf16[16,56,2560]{2,1,0:T(8,128)(2,1)S(1)}, bf16[16,56,2560]{2,1,0:T(8,128)(2,1)S(1)}, bf16[16,56,2560]{2,1,0:T(8,128)(2,1)S(1)}, bf16[16,56,25...) custom-call(bf16[2,16,56,2560]{3,2,1,0:T(8,128)(2,1)} %bitcast.9, ...), custom_call_target="tpu_custom_call" | custom-call | tf_op jit(solution)/shard_map/pallas_call | solution.py:244
  279.3 11.3 %shard_map.188 = (bf16[2,16,56,2560]{3,2,1,0:T(8,128)(2,1)}, bf16[2,16,56,2560]{3,2,1,0:T(8,128)(2,1)}, bf16[2,16,160,896]{3,2,1,0:T(8,128)(2,1)}, f32[2,56,2560...) custom-call(bf16[16,56,2560]{2,1,0:T(8,128)(2,1)S(1)} %get-tuple-ele, ...), custom_call_target="tpu_custom_call" | custom-call | tf_op jit(solution)/shard_map/pallas_call | solution.py:267

commit v5 on v4

--- a/solution.py
+++ b/solution.py
@@ -8,6 +8,7 @@
 from jax.experimental.pallas import tpu as pltpu
 from jax.sharding import PartitionSpec as P
 
+
 MESH = pl.DeviceIdType.MESH
 F32, BF16 = jnp.float32, jnp.bfloat16
 
@@ -30,10 +31,11 @@
 def kernel(n, count, *refs):
     g, w, m_in, v_in = (refs[i : i + 3] for i in range(0, 12, 3))
     layers, chips = g[0].shape[0], n // 2
-    new = [refs[12 + k * layers : 12 + (k + 1) * layers] for k in range(3)]
-    refs = refs[12 + 3 * layers :]
+    by_layer = lambda refs: [refs[k * layers : (k + 1) * layers] for k in range(3)]
+    fresh, refs = by_layer(refs[12:]), refs[12 + 3 * layers :]
     m, v, own, held = (refs[i : i + 3] for i in range(0, 12, 3))
-    (squares, own_sem, held_sem, pair_send, pair_recv, ring_send, ring_recv, hand_send, hand_recv, norm_send, norm_recv) = refs[12:]
+    new, refs = by_layer(refs[12:]), refs[12 + 3 * layers :]
+    (squares, own_sem, held_sem, pair_send, pair_recv, ring_send, ring_recv, norm_send, norm_recv) = refs
     pieces = [(k, l, first, rows) for k, first, rows in cuts([one.shape[1:] for one in held]) for l in range(layers)]
     weights = range(3)
     me = lax.axis_index("dp")
@@ -69,17 +71,7 @@
     def ring_copy(i, stage):
         k, l, first, rows = pieces[i]
         c, at = chunk(l, stage), pl.ds(first, rows)
-        return remote(own[k].at[l, c, at], new[k][l].at[2 * c + h, at], ring_send.at[k], ring_recv.at[stage, i], onward[l])
-
-    def gather_copy(i, c, step):
-        k, l, first, rows = pieces[i]
-        block = new[k][l].at[2 * c + h, pl.ds(first, rows)]
-        return remote(block, block, ring_send.at[k], ring_recv.at[step, i], onward[l])
-
-    def hand_copy(i, c):
-        k, l, first, rows = pieces[i]
-        block = new[k][l].at[2 * c + h, pl.ds(first, rows)]
-        return remote(block, block, hand_send.at[k], hand_recv.at[k], partner)
+        return remote(own[k].at[l, c, at], new[k][l].at[2 * c + h, at], ring_send.at[k], ring_recv.at[lax.rem(stage, 3), i], onward[l])
 
     def state_copies(k):
         return [
@@ -88,9 +80,9 @@
             pltpu.make_async_copy(w[k].at[:, me], held[k], held_sem.at[6 + k]),
         ]
 
-    def all_of(k, stages, send, recv):
+    def all_of(k, stages, send):
         block = own[k].at[:, pl.ds(0, stages)]
-        return remote(block, block, send.at[k], recv.at[k], partner)
+        return remote(block, block, send.at[k], send.at[k], partner)
 
     def add(i, stage, arrived, total=0, squared=False):
         k, l, first, rows = pieces[i]
@@ -134,7 +126,7 @@
         add(i, 0, False)
         ring_copy(i, 0).start()
     for k in weights:
-        all_of(k, 1, pair_send, hand_recv).wait_send()
+        all_of(k, 1, pair_send).wait_send()
     for i in everyone:
         own_copy(i, 1).start()
         pair_copy(i, 1).start()
@@ -169,8 +161,8 @@
     for k in weights:
         for copy in state_copies(k):
             copy.wait()
-        all_of(k, last, ring_send, hand_recv).wait_send()
-        all_of(k, last, pair_send, hand_recv).wait_send()
+        all_of(k, last, ring_send).wait_send()
+        all_of(k, last, pair_send).wait_send()
     others = squares.at[pl.ds(0, n - 1)]
     remote(others, others, norm_send, norm_recv, partner).wait_recv()
     everything = jnp.sum(jnp.sum(squares[...], axis=0), axis=1, keepdims=True)
@@ -188,38 +180,33 @@
             old = held[k][l, at, :].astype(F32)
             m[k][l, at, :] = m_new
             v[k][l, at, :] = v_new
-            new[k][l][me, at, :] = (old - 0.02 * (m_new * lax.rsqrt(v_new + 1e-8) + 0.1 * old)).astype(BF16)
+            fresh[k][l][at, :] = (old - 0.02 * (m_new * lax.rsqrt(v_new + 1e-8) + 0.1 * old)).astype(BF16)
             return 0
 
         lax.fori_loop(0, rows // tile, body, 0)
-        gather_copy(i, z, 0).start()
-        hand_copy(i, z).start()
-
-    def forward(step, _):
-        for i in everyone:
-            c = chunk(pieces[i][1], step)
-            gather_copy(i, c, step).wait_recv()
-            gather_copy(i, c, step + 1).start()
-            hand_copy(i, c).start()
-        return 0
-
-    lax.fori_loop(0, last - 1, forward, 0)
-    for i in everyone:
-        c = chunk(pieces[i][1], last - 1)
-        gather_copy(i, c, last - 1).wait_recv()
-        hand_copy(i, c).start()
     remote(others, others, norm_send, norm_recv, partner).wait_send()
-    for k in weights:
-        all_of(k, last, ring_send, hand_recv).wait_send()
-    for k in weights:
-        all_of(k, chips, hand_send, hand_recv).wait()
-
-
-def put_out(layers, *refs):
-    new, moments = refs[: 3 * layers], refs[3 * layers : 3 * layers + 6]
-    outs, sem = refs[3 * layers + 6 : -1], refs[-1]
-    pairs = [(one, outs[i // layers].at[i % layers]) for i, one in enumerate(new)] + list(zip(moments, outs[3:]))
-    copies = [pltpu.make_async_copy(one, out, sem.at[i]) for i, (one, out) in enumerate(pairs)]
+
+
+def put_out(*refs):
+    half = len(refs) // 2
+    copies = [pltpu.make_async_copy(refs[i], refs[half + i], refs[-1].at[i]) for i in range(half)]
+    for copy in copies:
+        copy.start()
+    for copy in copies:
+        copy.wait()
+
+
+def place(n, step, layers, *refs):
+    blocks, out, sem = refs[: 2 * layers], refs[-2], refs[-1]
+    chips = n // 2
+    me = lax.axis_index("dp")
+    h, z = lax.rem(me, 2), lax.div(me, 2)
+    copies = []
+    for i, block in enumerate(blocks):
+        l = i % layers
+        c = lax.rem(z + chips - step, chips) if l == 0 else lax.rem(z + step, chips)
+        row = 2 * c + (h if i < layers else 1 - h)
+        copies.append(pltpu.make_async_copy(block, out.at[l, row], sem.at[i]))
     for copy in copies:
         copy.start()
     for copy in copies:
@@ -239,15 +226,17 @@
         weights = [cut(t, part) for t, part in zip(weights, parts)]
         chips, pieces = n // 2, layers * len(cuts(parts))
         sem = pltpu.SemaphoreType.DMA
-        outs = [pltpu.VMEM((n, *part), BF16) for part in parts for _ in range(layers)] + [pltpu.VMEM((layers, *part), F32) for part in parts] * 2
-        grant = 24 * 1024 * 1024
+        vmem, hbm = pl.BlockSpec(memory_space=pltpu.VMEM), pl.BlockSpec(memory_space=pltpu.HBM)
+        outs = [pltpu.VMEM(part, BF16) for part in parts for _ in range(layers)] + [pltpu.VMEM((layers, *part), F32) for part in parts] * 2
+        grant = 44 * 1024 * 1024
         result = pl.pallas_call(
             functools.partial(kernel, n, count),
             out_shape=outs,
-            in_specs=[pl.BlockSpec(memory_space=pltpu.HBM)] * 12,
-            out_specs=[pl.BlockSpec(memory_space=pltpu.VMEM)] * len(outs),
+            in_specs=[hbm] * 12,
+            out_specs=[vmem] * len(outs),
             scratch_shapes=[pltpu.VMEM((layers, chips, *part), BF16) for part in parts]
             + [pltpu.VMEM((layers, *part), BF16) for part in parts]
+            + [pltpu.VMEM((n, *part), BF16) for part in parts for _ in range(layers)]
             + [
                 pltpu.VMEM((n, 1, 128), F32),
                 sem((pieces,)),
@@ -255,25 +244,45 @@
                 sem((3,)),
                 sem((2, pieces)),
                 sem((3,)),
-                sem((chips - 1, pieces)),
-                sem((3,)),
-                sem((3,)),
+                sem((3, pieces)),
                 sem,
                 sem,
             ],
             compiler_params=pltpu.CompilerParams(collective_id=0, has_side_effects=True, vmem_limit_bytes=grant),
         )(*(pltpu.with_memory_space_constraint(one, pltpu.HBM) for one in (*terms, *weights, *m, *v)))
-        result = [pltpu.with_memory_space_constraint(one, pltpu.VMEM) for one in result]
-        result = pl.pallas_call(
-            functools.partial(put_out, layers),
-            out_shape=[pltpu.HBM((layers, n, *part), BF16) for part in parts] + [pltpu.HBM((layers, *part), F32) for part in parts] * 2,
-            in_specs=[pl.BlockSpec(memory_space=pltpu.VMEM)] * len(result),
-            out_specs=[pl.BlockSpec(memory_space=pltpu.HBM)] * 9,
-            scratch_shapes=[sem((len(result),))],
+        moments = result[3 * layers :]
+        moments = pl.pallas_call(
+            put_out,
+            out_shape=[pltpu.HBM(one.shape, one.dtype) for one in moments],
+            in_specs=[vmem] * len(moments),
+            out_specs=[hbm] * len(moments),
+            scratch_shapes=[sem((len(moments),))],
+            cost_estimate=pl.CostEstimate(flops=0, bytes_accessed=sum(2 * 4 * one.size for one in moments), transcendentals=0),
             compiler_params=pltpu.CompilerParams(vmem_limit_bytes=grant),
-        )(*result)
-        whole = [one.reshape(layers, -1, one.shape[-1]) for one in result[:3]]
-        return (*whole, *result[3:])
+        )(*(pltpu.with_memory_space_constraint(one, pltpu.VMEM) for one in moments))
+
+        onward = [[(i, (i + 2) % n) for i in range(n)], [(i, (i - 2) % n) for i in range(n)]]
+        other = [(i, i + 1 - 2 * (i % 2)) for i in range(n)]
+        held = [result[k * layers : (k + 1) * layers] for k in range(3)]
+        whole = [None] * 3
+        for at in range(chips):
+            for k in range(3):
+                handed = [lax.ppermute(one, "dp", other) for one in held[k]]
+                args = [*held[k], *handed] + ([whole[k]] if at else [])
+                whole[k] = pl.pallas_call(
+                    functools.partial(place, n, at, layers),
+                    out_shape=pltpu.HBM((layers, n, *parts[k]), BF16),
+                    in_specs=[vmem] * (2 * layers) + [hbm] * bool(at),
+                    out_specs=hbm,
+                    scratch_shapes=[sem((2 * layers,))],
+                    input_output_aliases={2 * layers: 0} if at else {},
+                    cost_estimate=pl.CostEstimate(flops=0, bytes_accessed=8 * layers * math.prod(parts[k]), transcendentals=0),
+                    compiler_params=pltpu.CompilerParams(has_side_effects=True, vmem_limit_bytes=8 * 1024 * 1024),
+                )(*args)
+                if at + 1 < chips:
+                    held[k] = [lax.ppermute(one, "dp", onward[l]) for l, one in enumerate(held[k])]
+        whole = [one.reshape(layers, -1, one.shape[-1]) for one in whole]
+        return (*whole, *moments)
 
     all_of, cut = P(None, None, None), P(None, "dp", None)
     return jax.shard_map(

time: 291 us -> 333 us (1.14)
  Pallas kernels: 290 us -> 179 us
  starting transfers between devices: 0 us -> 67.8 us
  waiting for transfers between devices: 0 us -> 48.6 us
  local copies, waits for them, and re-layouts: 0 us -> 35.3 us
    pallas_call x1, Pallas kernels: 279 us -> 148 us  [step(): pl.pallas_call(functools.partial(kernel, n, count), out_shape=outs, in_sp...]
    ppermute x0 -> x90, starting transfers between devices: none -> 67.8 us  [the longest x48 41 us: step(): handed = [lax.ppermute(one, 'dp', other) for one in held[k]]]
    ppermute x0 -> x90, waiting for transfers between devices: none -> 48.6 us  [the longest x42 48.5 us: step(): lax.ppermute(one, 'dp', onward[l])]
    unnamed x0 -> x152, local copies, waits for them, and re-layouts: none -> 35.3 us
    pallas_call x1 -> x25, Pallas kernels: 11.3 us -> 31.4 us  [the longest x24 28.5 us: step(): pl.pallas_call(functools.partial(place, n, at, layers), out_shape=pltpu.H...]
  transfers between devices with their start and end apart: 0 -> 90, of which waited for: 0 -> 30; matrix products, arithmetic and copies ran while one was open for 0% -> 0% of each run, Pallas kernels for 0% -> 9%
where the time goes in v5:
time: 333 us; the launch traced here: 332 us
  Pallas kernels  179 us (54%)
  starting transfers between devices  67.8 us (20%)
  waiting for transfers between devices  48.6 us (15%)
  local copies, waits for them, and re-layouts  35.3 us (11%)
    pallas_call x1, Pallas kernels, step(): pl.pallas_call(functools.partial(kernel, n, count), out_shape=outs, in_sp...  148 us
    ppermute x42, waiting for transfers between devices, step(): lax.ppermute(one, 'dp', onward[l])  48.5 us
    ppermute x48, starting transfers between devices, step(): handed = [lax.ppermute(one, 'dp', other) for one in held[k]]  41 us
    unnamed x152, local copies, waits for them, and re-layouts  35.3 us
    pallas_call x24, Pallas kernels, step(): pl.pallas_call(functools.partial(place, n, at, layers), out_shape=pltpu.H...  28.5 us
    ppermute x42, starting transfers between devices, step(): lax.ppermute(one, 'dp', onward[l])  26.9 us
  transfers between devices with their start and end apart: 90, of which 30 were waited for; matrix products, arithmetic and copies ran while one was open for 0% of the time, Pallas kernels for 9%

profile of v5, /device:TPU:21, one launch (start us, length us, event | category | flops | bytes accessed | tf_op | source)
XLA Modules:
  0.0 332.2 jit_solution(4186707197068721434)
XLA Ops:
  0.6 147.6 %shard_map.187 = (bf16[56,2560]{1,0:T(8,128)(2,1)S(1)}, bf16[56,2560]{1,0:T(8,128)(2,1)S(1)}, bf16[56,2560]{1,0:T(8,128)(2,1)S(1)}, bf16[56,2560]{1,0:T(8,128)(2...) custom-call(bf16[2,16,56,2560]{3,2,1,0:T(8,128)(2,1)} %bitcast.12, ...), custom_call_target="tpu_custom_call" | custom-call | tf_op jit(solution)/shard_map/pallas_call | solution.py:232
  150.5 2.1 collective-permute-start.67
  156.4 2.0 collective-permute-done.60.refs_0_
  169.7 2.4 collective-permute-done.refs_0_
  175.3 3.4 %collective-permute-done.61.refs_0_ = bf16[160,896]{1,0:T(8,128)(2,1)S(1)} collective-permute-done((bf16[160,896]{1,0:T(8,128)(2,1)S(1)}, bf16[160,896]{1,0:T(8,128)(2,1)S(1)}, u32[]{:S(2)}, u32[]{:S(2)}) %collective-permute-start.61) | collective-permute-done | bytes 286752 | tf_op jit(solution)/shard_map/ppermute | solution.py:283
  179.2 2.2 collective-permute-start.26
  182.9 2.0 collective-permute-done.31.refs_0_
  185.7 2.2 collective-permute-start.84
  188.6 3.0 collective-permute-done.1.refs_0_
  191.9 2.2 collective-permute-start.54
  194.2 3.0 collective-permute-done.62.refs_0_
  199.0 2.1 collective-permute-start.24
  201.3 2.1 collective-permute-done.32.refs_0_
  205.2 2.1 collective-permute-start.82
  207.4 3.0 collective-permute-done.2.refs_0_
  213.8 2.8 collective-permute-done.63.refs_0_
  217.6 2.1 collective-permute-start.22
  220.0 3.1 collective-permute-done.33.refs_0_
  223.5 2.3 collective-permute-start.80
  226.0 3.0 collective-permute-done.3.refs_0_
  230.6 2.0 collective-permute-start.50
  232.7 2.4 collective-permute-done.64.refs_0_
  236.6 2.1 collective-permute-start.20
  239.5 2.4 collective-permute-done.34.refs_0_
  242.8 1.9 collective-permute-start.78
  246.4 2.2 collective-permute-done.4.refs_0_
  249.0 2.1 collective-permute-start.48
  253.1 2.0 collective-permute-done.65.refs_0_
  292.1 2.9 shard_map.212
  325.4 2.1 shard_map.211
  327.5 2.3 shard_map.203
  329.8 2.3 shard_map.195
  (326 shorter events, 109.5 us)
Async XLA Ops:
  149.2 9.2 %collective-permute-start.60 = (bf16[160,896]{1,0:T(8,128)(2,1)S(1)}, bf16[160,896]{1,0:T(8,128)(2,1)S(1)}, u32[]{:S(2)}, u32[]{:S(2)}) collective-permute-start(bf16[160,896]{1,0:T(8,128)(2,1)S(1)} %get-tuple-element.31.refs_0_), channel_id=1, source_target_pairs={{0,2},{1,3},{2,4},{3,5},{4,6},{5,7},{6,8},{7,9},{8,10},{9,11},{10,... | collective-permute-start | bytes 860168 | tf_op jit(solution)/shard_map/ppermute | solution.py:283
  150.5 9.6 %collective-permute-start.67 = (bf16[160,896]{1,0:T(8,128)(2,1)S(1)}, bf16[160,896]{1,0:T(8,128)(2,1)S(1)}, u32[]{:S(2)}, u32[]{:S(2)}) collective-permute-start(bf16[160,896]{1,0:T(8,128)(2,1)S(1)} %get-tuple-element.32.refs_1_), channel_id=1, source_target_pairs={{0,14},{1,15},{2,0},{3,1},{4,2},{5,3},{6,4},{7,5},{8,6},{9,7},{10,... | collective-permute-start | bytes 860168 | tf_op jit(solution)/shard_map/ppermute | solution.py:283
  155.0 10.1 %collective-permute-start.30 = (bf16[56,2560]{1,0:T(8,128)(2,1)S(1)}, bf16[56,2560]{1,0:T(8,128)(2,1)S(1)}, u32[]{:S(2)}, u32[]{:S(2)}) collective-permute-start(bf16[56,2560]{1,0:T(8,128)(2,1)S(1)} %get-tuple-element.29.refs_0_), channel_id=1, source_target_pairs={{0,2},{1,3},{2,4},{3,5},{4,6},{5,7},{6,8},{7,9},{8,10},{9,11},{10,... | collective-permute-start | bytes 860168 | tf_op jit(solution)/shard_map/ppermute | solution.py:283
  163.0 9.1 %collective-permute-start = (bf16[56,2560]{1,0:T(8,128)(2,1)S(1)}, bf16[56,2560]{1,0:T(8,128)(2,1)S(1)}, u32[]{:S(2)}, u32[]{:S(2)}) collective-permute-start(bf16[56,2560]{1,0:T(8,128)(2,1)S(1)} %get-tuple-element.27.refs_0_), channel_id=1, source_target_pairs={{0,2},{1,3},{2,4},{3,5},{4,6},{5,7},{6,8},{7,9},{8,10},{9,11},{10,... | collective-permute-start | bytes 860168 | tf_op jit(solution)/shard_map/ppermute | solution.py:283
  169.6 9.1 %collective-permute-start.61 = (bf16[160,896]{1,0:T(8,128)(2,1)S(1)}, bf16[160,896]{1,0:T(8,128)(2,1)S(1)}, u32[]{:S(2)}, u32[]{:S(2)}) collective-permute-start(bf16[160,896]{1,0:T(8,128)(2,1)S(1)} %collective-permute-done.60.refs_0_), channel_id=1, source_target_pairs={{0,2},{1,3},{2,4},{3,5},{4,6},{5,7},{6,8},{7,9},{8,10},{9,11},{10,... | collective-permute-start | bytes 860168 | tf_op jit(solution)/shard_map/ppermute | solution.py:283
  174.3 10.6 %collective-permute-start.31 = (bf16[56,2560]{1,0:T(8,128)(2,1)S(1)}, bf16[56,2560]{1,0:T(8,128)(2,1)S(1)}, u32[]{:S(2)}, u32[]{:S(2)}) collective-permute-start(bf16[56,2560]{1,0:T(8,128)(2,1)S(1)} %collective-permute-done.30.refs_0_), channel_id=1, source_target_pairs={{0,2},{1,3},{2,4},{3,5},{4,6},{5,7},{6,8},{7,9},{8,10},{9,11},{10,... | collective-permute-start | bytes 860168 | tf_op jit(solution)/shard_map/ppermute | solution.py:283
  179.2 8.8 %collective-permute-start.26 = (bf16[56,2560]{1,0:T(8,128)(2,1)S(1)}, bf16[56,2560]{1,0:T(8,128)(2,1)S(1)}, u32[]{:S(2)}, u32[]{:S(2)}) collective-permute-start(bf16[56,2560]{1,0:T(8,128)(2,1)S(1)} %collective-permute-done.refs_0_), channel_id=1, source_target_pairs={{0,1},{1,0},{2,3},{3,2},{4,5},{5,4},{6,7},{7,6},{8,9},{9,8},{10,11... | collective-permute-start | bytes 860168 | tf_op jit(solution)/shard_map/ppermute | solution.py:270
  181.3 10.2 %collective-permute-start.1 = (bf16[56,2560]{1,0:T(8,128)(2,1)S(1)}, bf16[56,2560]{1,0:T(8,128)(2,1)S(1)}, u32[]{:S(2)}, u32[]{:S(2)}) collective-permute-start(bf16[56,2560]{1,0:T(8,128)(2,1)S(1)} %collective-permute-done.refs_0_), channel_id=1, source_target_pairs={{0,2},{1,3},{2,4},{3,5},{4,6},{5,7},{6,8},{7,9},{8,10},{9,11},{10,... | collective-permute-start | bytes 860168 | tf_op jit(solution)/shard_map/ppermute | solution.py:283
  188.0 9.3 %collective-permute-start.62 = (bf16[160,896]{1,0:T(8,128)(2,1)S(1)}, bf16[160,896]{1,0:T(8,128)(2,1)S(1)}, u32[]{:S(2)}, u32[]{:S(2)}) collective-permute-start(bf16[160,896]{1,0:T(8,128)(2,1)S(1)} %collective-permute-done.61.refs_0_), channel_id=1, source_target_pairs={{0,2},{1,3},{2,4},{3,5},{4,6},{5,7},{6,8},{7,9},{8,10},{9,11},{10,... | collective-permute-start | bytes 860168 | tf_op jit(solution)/shard_map/ppermute | solution.py:283
  191.9 9.2 %collective-permute-start.54 = (bf16[56,2560]{1,0:T(8,128)(2,1)S(1)}, bf16[56,2560]{1,0:T(8,128)(2,1)S(1)}, u32[]{:S(2)}, u32[]{:S(2)}) collective-permute-start(bf16[56,2560]{1,0:T(8,128)(2,1)S(1)} %collective-permute-done.31.refs_0_), channel_id=1, source_target_pairs={{0,1},{1,0},{2,3},{3,2},{4,5},{5,4},{6,7},{7,6},{8,9},{9,8},{10,11... | collective-permute-start | bytes 860168 | tf_op jit(solution)/shard_map/ppermute | solution.py:270
  194.1 9.3 %collective-permute-start.32 = (bf16[56,2560]{1,0:T(8,128)(2,1)S(1)}, bf16[56,2560]{1,0:T(8,128)(2,1)S(1)}, u32[]{:S(2)}, u32[]{:S(2)}) collective-permute-start(bf16[56,2560]{1,0:T(8,128)(2,1)S(1)} %collective-permute-done.31.refs_0_), channel_id=1, source_target_pairs={{0,2},{1,3},{2,4},{3,5},{4,6},{5,7},{6,8},{7,9},{8,10},{9,11},{10,... | collective-permute-start | bytes 860168 | tf_op jit(solution)/shard_map/ppermute | solution.py:283
  201.1 9.3 %collective-permute-start.2 = (bf16[56,2560]{1,0:T(8,128)(2,1)S(1)}, bf16[56,2560]{1,0:T(8,128)(2,1)S(1)}, u32[]{:S(2)}, u32[]{:S(2)}) collective-permute-start(bf16[56,2560]{1,0:T(8,128)(2,1)S(1)} %collective-permute-done.1.refs_0_), channel_id=1, source_target_pairs={{0,2},{1,3},{2,4},{3,5},{4,6},{5,7},{6,8},{7,9},{8,10},{9,11},{10,... | collective-permute-start | bytes 860168 | tf_op jit(solution)/shard_map/ppermute | solution.py:283
  207.3 9.3 %collective-permute-start.63 = (bf16[160,896]{1,0:T(8,128)(2,1)S(1)}, bf16[160,896]{1,0:T(8,128)(2,1)S(1)}, u32[]{:S(2)}, u32[]{:S(2)}) collective-permute-start(bf16[160,896]{1,0:T(8,128)(2,1)S(1)} %collective-permute-done.62.refs_0_), channel_id=1, source_target_pairs={{0,2},{1,3},{2,4},{3,5},{4,6},{5,7},{6,8},{7,9},{8,10},{9,11},{10,... | collective-permute-start | bytes 860168 | tf_op jit(solution)/shard_map/ppermute | solution.py:283
  213.2 9.9 %collective-permute-start.33 = (bf16[56,2560]{1,0:T(8,128)(2,1)S(1)}, bf16[56,2560]{1,0:T(8,128)(2,1)S(1)}, u32[]{:S(2)}, u32[]{:S(2)}) collective-permute-start(bf16[56,2560]{1,0:T(8,128)(2,1)S(1)} %collective-permute-done.32.refs_0_), channel_id=1, source_target_pairs={{0,2},{1,3},{2,4},{3,5},{4,6},{5,7},{6,8},{7,9},{8,10},{9,11},{10,... | collective-permute-start | bytes 860168 | tf_op jit(solution)/shard_map/ppermute | solution.py:283
  219.7 9.3 %collective-permute-start.3 = (bf16[56,2560]{1,0:T(8,128)(2,1)S(1)}, bf16[56,2560]{1,0:T(8,128)(2,1)S(1)}, u32[]{:S(2)}, u32[]{:S(2)}) collective-permute-start(bf16[56,2560]{1,0:T(8,128)(2,1)S(1)} %collective-permute-done.2.refs_0_), channel_id=1, source_target_pairs={{0,2},{1,3},{2,4},{3,5},{4,6},{5,7},{6,8},{7,9},{8,10},{9,11},{10,... | collective-permute-start | bytes 860168 | tf_op jit(solution)/shard_map/ppermute | solution.py:283
  223.5 9.1 %collective-permute-start.80 = (bf16[160,896]{1,0:T(8,128)(2,1)S(1)}, bf16[160,896]{1,0:T(8,128)(2,1)S(1)}, u32[]{:S(2)}, u32[]{:S(2)}) collective-permute-start(bf16[160,896]{1,0:T(8,128)(2,1)S(1)} %collective-permute-done.63.refs_0_), channel_id=1, source_target_pairs={{0,1},{1,0},{2,3},{3,2},{4,5},{5,4},{6,7},{7,6},{8,9},{9,8},{10,11... | collective-permute-start | bytes 860168 | tf_op jit(solution)/shard_map/ppermute | solution.py:270
  225.8 9.3 %collective-permute-start.64 = (bf16[160,896]{1,0:T(8,128)(2,1)S(1)}, bf16[160,896]{1,0:T(8,128)(2,1)S(1)}, u32[]{:S(2)}, u32[]{:S(2)}) collective-permute-start(bf16[160,896]{1,0:T(8,128)(2,1)S(1)} %collective-permute-done.63.refs_0_), channel_id=1, source_target_pairs={{0,2},{1,3},{2,4},{3,5},{4,6},{5,7},{6,8},{7,9},{8,10},{9,11},{10,... | collective-permute-start | bytes 860168 | tf_op jit(solution)/shard_map/ppermute | solution.py:283
  232.6 9.3 %collective-permute-start.34 = (bf16[56,2560]{1,0:T(8,128)(2,1)S(1)}, bf16[56,2560]{1,0:T(8,128)(2,1)S(1)}, u32[]{:S(2)}, u32[]{:S(2)}) collective-permute-start(bf16[56,2560]{1,0:T(8,128)(2,1)S(1)} %collective-permute-done.33.refs_0_), channel_id=1, source_target_pairs={{0,2},{1,3},{2,4},{3,5},{4,6},{5,7},{6,8},{7,9},{8,10},{9,11},{10,... | collective-permute-start | bytes 860168 | tf_op jit(solution)/shard_map/ppermute | solution.py:283
  239.5 9.1 %collective-permute-start.4 = (bf16[56,2560]{1,0:T(8,128)(2,1)S(1)}, bf16[56,2560]{1,0:T(8,128)(2,1)S(1)}, u32[]{:S(2)}, u32[]{:S(2)}) collective-permute-start(bf16[56,2560]{1,0:T(8,128)(2,1)S(1)} %collective-permute-done.3.refs_0_), channel_id=1, source_target_pairs={{0,2},{1,3},{2,4},{3,5},{4,6},{5,7},{6,8},{7,9},{8,10},{9,11},{10,... | collective-permute-start | bytes 860168 | tf_op jit(solution)/shard_map/ppermute | solution.py:283
  246.1 9.1 %collective-permute-start.65 = (bf16[160,896]{1,0:T(8,128)(2,1)S(1)}, bf16[160,896]{1,0:T(8,128)(2,1)S(1)}, u32[]{:S(2)}, u32[]{:S(2)}) collective-permute-start(bf16[160,896]{1,0:T(8,128)(2,1)S(1)} %collective-permute-done.64.refs_0_), channel_id=1, source_target_pairs={{0,2},{1,3},{2,4},{3,5},{4,6},{5,7},{6,8},{7,9},{8,10},{9,11},{10,... | collective-permute-start | bytes 860168 | tf_op jit(solution)/shard_map/ppermute | solution.py:283
  249.0 9.1 %collective-permute-start.48 = (bf16[56,2560]{1,0:T(8,128)(2,1)S(1)}, bf16[56,2560]{1,0:T(8,128)(2,1)S(1)}, u32[]{:S(2)}, u32[]{:S(2)}) collective-permute-start(bf16[56,2560]{1,0:T(8,128)(2,1)S(1)} %collective-permute-done.34.refs_0_), channel_id=1, source_target_pairs={{0,1},{1,0},{2,3},{3,2},{4,5},{5,4},{6,7},{7,6},{8,9},{9,8},{10,11... | collective-permute-start | bytes 860168 | tf_op jit(solution)/shard_map/ppermute | solution.py:270
  252.6 9.1 %collective-permute-start.35 = (bf16[56,2560]{1,0:T(8,128)(2,1)S(1)}, bf16[56,2560]{1,0:T(8,128)(2,1)S(1)}, u32[]{:S(2)}, u32[]{:S(2)}) collective-permute-start(bf16[56,2560]{1,0:T(8,128)(2,1)S(1)} %collective-permute-done.34.refs_0_), channel_id=1, source_target_pairs={{0,2},{1,3},{2,4},{3,5},{4,6},{5,7},{6,8},{7,9},{8,10},{9,11},{10,... | collective-permute-start | bytes 860168 | tf_op jit(solution)/shard_map/ppermute | solution.py:283
  259.6 9.1 %collective-permute-start.5 = (bf16[56,2560]{1,0:T(8,128)(2,1)S(1)}, bf16[56,2560]{1,0:T(8,128)(2,1)S(1)}, u32[]{:S(2)}, u32[]{:S(2)}) collective-permute-start(bf16[56,2560]{1,0:T(8,128)(2,1)S(1)} %collective-permute-done.4.refs_0_), channel_id=1, source_target_pairs={{0,2},{1,3},{2,4},{3,5},{4,6},{5,7},{6,8},{7,9},{8,10},{9,11},{10,... | collective-permute-start | bytes 860168 | tf_op jit(solution)/shard_map/ppermute | solution.py:283
  266.2 9.1 %collective-permute-start.66 = (bf16[160,896]{1,0:T(8,128)(2,1)S(1)}, bf16[160,896]{1,0:T(8,128)(2,1)S(1)}, u32[]{:S(2)}, u32[]{:S(2)}) collective-permute-start(bf16[160,896]{1,0:T(8,128)(2,1)S(1)} %collective-permute-done.65.refs_0_), channel_id=1, source_target_pairs={{0,2},{1,3},{2,4},{3,5},{4,6},{5,7},{6,8},{7,9},{8,10},{9,11},{10,... | collective-permute-start | bytes 860168 | tf_op jit(solution)/shard_map/ppermute | solution.py:283
  272.8 9.2 %collective-permute-start.36 = (bf16[56,2560]{1,0:T(8,128)(2,1)S(1)}, bf16[56,2560]{1,0:T(8,128)(2,1)}, u32[]{:S(2)}, u32[]{:S(2)}) collective-permute-start(bf16[56,2560]{1,0:T(8,128)(2,1)S(1)} %collective-permute-done.35.refs_0_), channel_id=1, source_target_pairs={{0,2},{1,3},{2,4},{3,5},{4,6},{5,7},{6,8},{7,9},{8,10},{9,11},{10,... | collective-permute-start | bytes 860168 | tf_op jit(solution)/shard_map/ppermute | solution.py:283
  276.9 9.0 %collective-permute-start.16 = (bf16[56,2560]{1,0:T(8,128)(2,1)S(1)}, bf16[56,2560]{1,0:T(8,128)(2,1)S(1)}, u32[]{:S(2)}, u32[]{:S(2)}) collective-permute-start(bf16[56,2560]{1,0:T(8,128)(2,1)S(1)} %collective-permute-done.5.refs_0_), channel_id=1, source_target_pairs={{0,1},{1,0},{2,3},{3,2},{4,5},{5,4},{6,7},{7,6},{8,9},{9,8},{10,11... | collective-permute-start | bytes 860168 | tf_op jit(solution)/shard_map/ppermute | solution.py:270
  279.5 9.2 %collective-permute-start.6 = (bf16[56,2560]{1,0:T(8,128)(2,1)S(1)}, bf16[56,2560]{1,0:T(8,128)(2,1)}, u32[]{:S(2)}, u32[]{:S(2)}) collective-permute-start(bf16[56,2560]{1,0:T(8,128)(2,1)S(1)} %collective-permute-done.5.refs_0_), channel_id=1, source_target_pairs={{0,2},{1,3},{2,4},{3,5},{4,6},{5,7},{6,8},{7,9},{8,10},{9,11},{10,... | collective-permute-start | bytes 860168 | tf_op jit(solution)/shard_map/ppermute | solution.py:283
  286.6 38.4 %collective-permute-start.75 = (bf16[160,896]{1,0:T(8,128)(2,1)}, bf16[160,896]{1,0:T(8,128)(2,1)}, u32[]{:S(2)}, u32[]{:S(2)}) collective-permute-start(bf16[160,896]{1,0:T(8,128)(2,1)} %collective-permute-done.73.refs_1_), channel_id=1, source_target_pairs={{0,1},{1,0},{2,3},{3,2},{4,5},{5,4},{6,7},{7,6},{8,9},{9,8},{10,11... | collective-permute-start | bytes 860168 | tf_op jit(solution)/shard_map/ppermute | solution.py:270
  287.4 40.2 %collective-permute-start.44 = (bf16[56,2560]{1,0:T(8,128)(2,1)}, bf16[56,2560]{1,0:T(8,128)(2,1)}, u32[]{:S(2)}, u32[]{:S(2)}) collective-permute-start(bf16[56,2560]{1,0:T(8,128)(2,1)} %collective-permute-done.36.refs_0_), channel_id=1, source_target_pairs={{0,1},{1,0},{2,3},{3,2},{4,5},{5,4},{6,7},{7,6},{8,9},{9,8},{10,11... | collective-permute-start | bytes 860168 | tf_op jit(solution)/shard_map/ppermute | solution.py:270
  288.7 38.9 %collective-permute-start.45 = (bf16[56,2560]{1,0:T(8,128)(2,1)}, bf16[56,2560]{1,0:T(8,128)(2,1)}, u32[]{:S(2)}, u32[]{:S(2)}) collective-permute-start(bf16[56,2560]{1,0:T(8,128)(2,1)} %collective-permute-done.43.refs_1_), channel_id=1, source_target_pairs={{0,1},{1,0},{2,3},{3,2},{4,5},{5,4},{6,7},{7,6},{8,9},{9,8},{10,11... | collective-permute-start | bytes 860168 | tf_op jit(solution)/shard_map/ppermute | solution.py:270
  290.0 39.8 %collective-permute-start.14 = (bf16[56,2560]{1,0:T(8,128)(2,1)}, bf16[56,2560]{1,0:T(8,128)(2,1)}, u32[]{:S(2)}, u32[]{:S(2)}) collective-permute-start(bf16[56,2560]{1,0:T(8,128)(2,1)} %collective-permute-done.6.refs_0_), channel_id=1, source_target_pairs={{0,1},{1,0},{2,3},{3,2},{4,5},{5,4},{6,7},{7,6},{8,9},{9,8},{10,11... | collective-permute-start | bytes 860168 | tf_op jit(solution)/shard_map/ppermute | solution.py:270
  292.1 37.7 %collective-permute-start.15 = (bf16[56,2560]{1,0:T(8,128)(2,1)}, bf16[56,2560]{1,0:T(8,128)(2,1)}, u32[]{:S(2)}, u32[]{:S(2)}) collective-permute-start(bf16[56,2560]{1,0:T(8,128)(2,1)} %collective-permute-done.13.refs_1_), channel_id=1, source_target_pairs={{0,1},{1,0},{2,3},{3,2},{4,5},{5,4},{6,7},{7,6},{8,9},{9,8},{10,11... | collective-permute-start | bytes 860168 | tf_op jit(solution)/shard_map/ppermute | solution.py:270
  (134 other events, 509.0 us)

commit v6 on v5

--- a/solution.py
+++ b/solution.py
@@ -28,13 +28,39 @@
     return [(k, 0, small), *((i, 0, part[0]) for i, part in enumerate(most)), (k, small, rows - 2 * small), (k, rows - small, small)]
 
 
+def take_step(factor, g, w, m, v, w_new, m_new, v_new):
+    rows, columns = g.shape
+    tile = row_tile(rows, columns)
+
+    def body(j, _):
+        at = pl.ds(pl.multiple_of(j * tile, 8), tile)
+        x = g[at, :].astype(F32) * factor
+        one = 0.9 * m[at, :] + 0.1 * x
+        two = 0.95 * v[at, :] + 0.05 * x * x
+        old = w[at, :].astype(F32)
+        m_new[at, :] = one
+        v_new[at, :] = two
+        w_new[at, :] = (old - 0.02 * (one * lax.rsqrt(two + 1e-8) + 0.1 * old)).astype(BF16)
+        return 0
+
+    lax.fori_loop(0, rows // tile, body, 0)
+
+
+def later_step(layers, *refs):
+    g, w, m, v, scale = refs[:5]
+    w_new, (m_new, v_new) = refs[5 : 5 + layers], refs[5 + layers :]
+    for l in range(layers):
+        take_step(scale[:1, :1], g.at[l], w.at[l], m.at[l], v.at[l], w_new[l], m_new.at[l], v_new.at[l])
+
+
 def kernel(n, count, *refs):
     g, w, m_in, v_in = (refs[i : i + 3] for i in range(0, 12, 3))
     layers, chips = g[0].shape[0], n // 2
     by_layer = lambda refs: [refs[k * layers : (k + 1) * layers] for k in range(3)]
-    fresh, refs = by_layer(refs[12:]), refs[12 + 3 * layers :]
-    m, v, own, held = (refs[i : i + 3] for i in range(0, 12, 3))
-    new, refs = by_layer(refs[12:]), refs[12 + 3 * layers :]
+    fresh, refs = refs[12 : 12 + layers], refs[12 + layers :]
+    m, v = refs[:3], refs[3:6]
+    sums, scale, own, held = (None, *refs[6:8]), refs[10], refs[11:14], (refs[14], *refs[8:10])
+    new, refs = by_layer(refs[15:]), refs[15 + 3 * layers :]
     (squares, own_sem, held_sem, pair_send, pair_recv, ring_send, ring_recv, norm_send, norm_recv) = refs
     pieces = [(k, l, first, rows) for k, first, rows in cuts([one.shape[1:] for one in held]) for l in range(layers)]
     weights = range(3)
@@ -96,9 +122,13 @@
             if arrived:
                 x = x + new[k][l][2 * c + h, at, :].astype(F32)
             x = x.astype(BF16)
-            own[k][l, c, at, :] = x
             if not squared:
+                own[k][l, c, at, :] = x
                 return total
+            if k:
+                sums[k][l, at, :] = x
+            else:
+                own[k][l, c, at, :] = x
             y = x.astype(F32)
             y = y * y
             y = sum(y[:, j : j + 128] for j in range(0, columns, 128))
@@ -108,13 +138,13 @@
 
     everyone = range(len(pieces))
 
+    barrier = pltpu.get_barrier_semaphore()
+    for other in (up, down, partner):
+        pl.semaphore_signal(barrier, inc=1, device_id={"dp": other}, device_id_type=MESH)
+
     for i in everyone:
         held_copy(i).start()
         own_copy(i, 0).start()
-
-    barrier = pltpu.get_barrier_semaphore()
-    for other in (partner, up, down):
-        pl.semaphore_signal(barrier, inc=1, device_id={"dp": other}, device_id_type=MESH)
     pl.semaphore_wait(barrier, 3)
 
     for i in everyone:
@@ -168,22 +198,9 @@
     everything = jnp.sum(jnp.sum(squares[...], axis=0), axis=1, keepdims=True)
     factor = jnp.minimum(1.0, 0.5 * lax.rsqrt(everything / count + 1e-30))
 
-    for i in everyone:
-        k, l, first, rows = pieces[i]
-        tile = row_tile(rows, held[k].shape[-1])
-
-        def body(j, _):
-            at = pl.ds(pl.multiple_of(first + j * tile, 8), tile)
-            x = own[k][l, z, at, :].astype(F32) * factor
-            m_new = 0.9 * m[k][l, at, :] + 0.1 * x
-            v_new = 0.95 * v[k][l, at, :] + 0.05 * x * x
-            old = held[k][l, at, :].astype(F32)
-            m[k][l, at, :] = m_new
-            v[k][l, at, :] = v_new
-            fresh[k][l][at, :] = (old - 0.02 * (m_new * lax.rsqrt(v_new + 1e-8) + 0.1 * old)).astype(BF16)
-            return 0
-
-        lax.fori_loop(0, rows // tile, body, 0)
+    scale[...] = jnp.broadcast_to(factor, scale.shape)
+    for l in range(layers):
+        take_step(factor, own[0].at[l, z], held[0].at[l], m[0].at[l], v[0].at[l], fresh[l], m[0].at[l], v[0].at[l])
     remote(others, others, norm_send, norm_recv, partner).wait_send()
 
 
@@ -227,7 +244,8 @@
         chips, pieces = n // 2, layers * len(cuts(parts))
         sem = pltpu.SemaphoreType.DMA
         vmem, hbm = pl.BlockSpec(memory_space=pltpu.VMEM), pl.BlockSpec(memory_space=pltpu.HBM)
-        outs = [pltpu.VMEM(part, BF16) for part in parts for _ in range(layers)] + [pltpu.VMEM((layers, *part), F32) for part in parts] * 2
+        outs = [pltpu.VMEM(parts[0], BF16)] * layers + [pltpu.VMEM((layers, *part), F32) for part in parts] * 2
+        outs += [pltpu.VMEM((layers, *part), BF16) for part in parts[1:]] * 2 + [pltpu.VMEM((8, 128), F32)]
         grant = 44 * 1024 * 1024
         result = pl.pallas_call(
             functools.partial(kernel, n, count),
@@ -235,7 +253,7 @@
             in_specs=[hbm] * 12,
             out_specs=[vmem] * len(outs),
             scratch_shapes=[pltpu.VMEM((layers, chips, *part), BF16) for part in parts]
-            + [pltpu.VMEM((layers, *part), BF16) for part in parts]
+            + [pltpu.VMEM((layers, *parts[0]), BF16)]
             + [pltpu.VMEM((n, *part), BF16) for part in parts for _ in range(layers)]
             + [
                 pltpu.VMEM((n, 1, 128), F32),
@@ -250,7 +268,21 @@
             ],
             compiler_params=pltpu.CompilerParams(collective_id=0, has_side_effects=True, vmem_limit_bytes=grant),
         )(*(pltpu.with_memory_space_constraint(one, pltpu.HBM) for one in (*terms, *weights, *m, *v)))
-        moments = result[3 * layers :]
+        held, rest = [result[:layers]], result[layers:]
+        m, v, sums, old, scale = list(rest[:3]), list(rest[3:6]), rest[6:8], rest[8:10], rest[10]
+        in_vmem = lambda args: [pltpu.with_memory_space_constraint(one, pltpu.VMEM) for one in args]
+        for k in (1, 2):
+            state = pltpu.VMEM((layers, *parts[k]), F32)
+            *one, m[k], v[k] = pl.pallas_call(
+                functools.partial(later_step, layers),
+                out_shape=[pltpu.VMEM(parts[k], BF16)] * layers + [state] * 2,
+                in_specs=[vmem] * 5,
+                out_specs=[vmem] * (layers + 2),
+                cost_estimate=pl.CostEstimate(flops=0, bytes_accessed=22 * layers * math.prod(parts[k]), transcendentals=0),
+                compiler_params=pltpu.CompilerParams(vmem_limit_bytes=grant),
+            )(*in_vmem([sums[k - 1], old[k - 1], m[k], v[k], scale]))
+            held.append(one)
+        moments = [*m, *v]
         moments = pl.pallas_call(
             put_out,
             out_shape=[pltpu.HBM(one.shape, one.dtype) for one in moments],
@@ -259,11 +291,10 @@
             scratch_shapes=[sem((len(moments),))],
             cost_estimate=pl.CostEstimate(flops=0, bytes_accessed=sum(2 * 4 * one.size for one in moments), transcendentals=0),
             compiler_params=pltpu.CompilerParams(vmem_limit_bytes=grant),
-        )(*(pltpu.with_memory_space_constraint(one, pltpu.VMEM) for one in moments))
+        )(*in_vmem(moments))
 
         onward = [[(i, (i + 2) % n) for i in range(n)], [(i, (i - 2) % n) for i in range(n)]]
         other = [(i, i + 1 - 2 * (i % 2)) for i in range(n)]
-        held = [result[k * layers : (k + 1) * layers] for k in range(3)]
         whole = [None] * 3
         for at in range(chips):
             for k in range(3):

time: 333 us -> 332 us (level)
    unnamed x152 -> x156, local copies, waits for them, and re-layouts: 35.3 us -> 33.7 us
where the time goes in v6:
time: 332 us
  Pallas kernels  180 us (54%)
  starting transfers between devices  67.3 us (20%)
  waiting for transfers between devices  49.3 us (15%)
  local copies, waits for them, and re-layouts  33.7 us (10%)
    pallas_call x1, Pallas kernels, step(): pl.pallas_call(functools.partial(kernel, n, count), out_shape=outs, in_sp...  146 us
    ppermute x42, waiting for transfers between devices, step(): lax.ppermute(one, 'dp', onward[l])  49.2 us
    ppermute x48, starting transfers between devices, step(): handed = [lax.ppermute(one, 'dp', other) for one in held[k]]  43.5 us
    unnamed x156, local copies, waits for them, and re-layouts  33.7 us
    pallas_call x24, Pallas kernels, step(): pl.pallas_call(functools.partial(place, n, at, layers), out_shape=pltpu.H...  28.5 us
    ppermute x42, starting transfers between devices, step(): lax.ppermute(one, 'dp', onward[l])  23.9 us
  transfers between devices with their start and end apart: 90, of which 30 were waited for; matrix products, arithmetic and copies ran while one was open for 0% of the time, Pallas kernels for 9%

profile of v6, /device:TPU:21, one launch (start us, length us, event | category | flops | bytes accessed | tf_op | source)
XLA Modules:
  0.0 331.6 jit_solution(15278640273623889549)
XLA Ops:
  0.6 146.1 %shard_map.187 = (bf16[56,2560]{1,0:T(8,128)(2,1)S(1)}, bf16[56,2560]{1,0:T(8,128)(2,1)S(1)}, f32[2,56,2560]{2,1,0:T(8,128)S(1)}, f32[2,56,2560]{2,1,0:T(8,128)S...) custom-call(bf16[2,16,56,2560]{3,2,1,0:T(8,128)(2,1)} %bitcast.12, ...), custom_call_target="tpu_custom_call" | custom-call | tf_op jit(solution)/shard_map/pallas_call | solution.py:250
  149.7 2.1 collective-permute-start.67
  155.8 2.4 collective-permute-done.60.refs_0_
  165.0 2.4 collective-permute-start.86
  168.9 2.6 collective-permute-done.refs_0_
  171.7 1.8 collective-permute-start.56
  174.7 3.3 collective-permute-done.61.refs_0_
  178.5 2.6 collective-permute-start.26
  182.1 1.9 collective-permute-done.31.refs_0_
  184.7 2.5 collective-permute-start.84
  187.3 3.1 collective-permute-done.1.refs_0_
  191.1 2.2 collective-permute-start.54
  193.7 3.0 collective-permute-done.62.refs_0_
  197.5 2.2 collective-permute-start.24
  199.8 3.0 collective-permute-done.32.refs_0_
  203.8 2.1 collective-permute-start.82
  206.1 3.0 collective-permute-done.2.refs_0_
  210.1 2.0 collective-permute-start.52
  212.4 2.8 collective-permute-done.63.refs_0_
  216.2 2.1 collective-permute-start.22
  218.4 3.3 %collective-permute-done.33.refs_0_ = bf16[56,2560]{1,0:T(8,128)(2,1)S(1)} collective-permute-done((bf16[56,2560]{1,0:T(8,128)(2,1)S(1)}, bf16[56,2560]{1,0:T(8,128)(2,1)S(1)}, u32[]{:S(2)}, u32[]{:S(2)}) %collective-permute-start.33) | collective-permute-done | bytes 286752 | tf_op jit(solution)/shard_map/ppermute | solution.py:314
  222.4 2.1 collective-permute-start.80
  224.8 3.0 collective-permute-done.3.refs_0_
  228.9 2.1 collective-permute-start.50
  231.2 2.7 collective-permute-done.64.refs_0_
  235.1 2.1 collective-permute-start.20
  241.4 1.9 collective-permute-start.78
  244.8 3.0 collective-permute-done.4.refs_0_
  291.1 2.9 shard_map.214
  324.8 2.1 shard_map.213
  326.9 2.3 shard_map.204
  329.2 2.3 shard_map.195
  (332 shorter events, 107.2 us)
Async XLA Ops:
  148.7 9.5 %collective-permute-start.60 = (bf16[160,896]{1,0:T(8,128)(2,1)S(1)}, bf16[160,896]{1,0:T(8,128)(2,1)S(1)}, u32[]{:S(2)}, u32[]{:S(2)}) collective-permute-start(bf16[160,896]{1,0:T(8,128)(2,1)S(1)} %get-tuple-element.49.refs_0_), channel_id=1, source_target_pairs={{0,2},{1,3},{2,4},{3,5},{4,6},{5,7},{6,8},{7,9},{8,10},{9,11},{10,... | collective-permute-start | bytes 860168 | tf_op jit(solution)/shard_map/ppermute | solution.py:314
  149.7 9.8 %collective-permute-start.67 = (bf16[160,896]{1,0:T(8,128)(2,1)S(1)}, bf16[160,896]{1,0:T(8,128)(2,1)S(1)}, u32[]{:S(2)}, u32[]{:S(2)}) collective-permute-start(bf16[160,896]{1,0:T(8,128)(2,1)S(1)} %get-tuple-element.50.refs_1_), channel_id=1, source_target_pairs={{0,14},{1,15},{2,0},{3,1},{4,2},{5,3},{6,4},{7,5},{8,6},{9,7},{10,... | collective-permute-start | bytes 860168 | tf_op jit(solution)/shard_map/ppermute | solution.py:314
  154.2 10.1 %collective-permute-start.30 = (bf16[56,2560]{1,0:T(8,128)(2,1)S(1)}, bf16[56,2560]{1,0:T(8,128)(2,1)S(1)}, u32[]{:S(2)}, u32[]{:S(2)}) collective-permute-start(bf16[56,2560]{1,0:T(8,128)(2,1)S(1)} %get-tuple-element.43.refs_0_), channel_id=1, source_target_pairs={{0,2},{1,3},{2,4},{3,5},{4,6},{5,7},{6,8},{7,9},{8,10},{9,11},{10,... | collective-permute-start | bytes 860168 | tf_op jit(solution)/shard_map/ppermute | solution.py:314
  162.3 9.1 %collective-permute-start = (bf16[56,2560]{1,0:T(8,128)(2,1)S(1)}, bf16[56,2560]{1,0:T(8,128)(2,1)S(1)}, u32[]{:S(2)}, u32[]{:S(2)}) collective-permute-start(bf16[56,2560]{1,0:T(8,128)(2,1)S(1)} %get-tuple-element.36.refs_0_), channel_id=1, source_target_pairs={{0,2},{1,3},{2,4},{3,5},{4,6},{5,7},{6,8},{7,9},{8,10},{9,11},{10,... | collective-permute-start | bytes 860168 | tf_op jit(solution)/shard_map/ppermute | solution.py:314
  168.8 9.1 %collective-permute-start.61 = (bf16[160,896]{1,0:T(8,128)(2,1)S(1)}, bf16[160,896]{1,0:T(8,128)(2,1)S(1)}, u32[]{:S(2)}, u32[]{:S(2)}) collective-permute-start(bf16[160,896]{1,0:T(8,128)(2,1)S(1)} %collective-permute-done.60.refs_0_), channel_id=1, source_target_pairs={{0,2},{1,3},{2,4},{3,5},{4,6},{5,7},{6,8},{7,9},{8,10},{9,11},{10,... | collective-permute-start | bytes 860168 | tf_op jit(solution)/shard_map/ppermute | solution.py:314
  171.7 9.4 %collective-permute-start.56 = (bf16[56,2560]{1,0:T(8,128)(2,1)S(1)}, bf16[56,2560]{1,0:T(8,128)(2,1)S(1)}, u32[]{:S(2)}, u32[]{:S(2)}) collective-permute-start(bf16[56,2560]{1,0:T(8,128)(2,1)S(1)} %collective-permute-done.30.refs_0_), channel_id=1, source_target_pairs={{0,1},{1,0},{2,3},{3,2},{4,5},{5,4},{6,7},{7,6},{8,9},{9,8},{10,11... | collective-permute-start | bytes 860168 | tf_op jit(solution)/shard_map/ppermute | solution.py:301
  173.5 10.5 %collective-permute-start.31 = (bf16[56,2560]{1,0:T(8,128)(2,1)S(1)}, bf16[56,2560]{1,0:T(8,128)(2,1)S(1)}, u32[]{:S(2)}, u32[]{:S(2)}) collective-permute-start(bf16[56,2560]{1,0:T(8,128)(2,1)S(1)} %collective-permute-done.30.refs_0_), channel_id=1, source_target_pairs={{0,2},{1,3},{2,4},{3,5},{4,6},{5,7},{6,8},{7,9},{8,10},{9,11},{10,... | collective-permute-start | bytes 860168 | tf_op jit(solution)/shard_map/ppermute | solution.py:314
  178.5 8.7 %collective-permute-start.26 = (bf16[56,2560]{1,0:T(8,128)(2,1)S(1)}, bf16[56,2560]{1,0:T(8,128)(2,1)S(1)}, u32[]{:S(2)}, u32[]{:S(2)}) collective-permute-start(bf16[56,2560]{1,0:T(8,128)(2,1)S(1)} %collective-permute-done.refs_0_), channel_id=1, source_target_pairs={{0,1},{1,0},{2,3},{3,2},{4,5},{5,4},{6,7},{7,6},{8,9},{9,8},{10,11... | collective-permute-start | bytes 860168 | tf_op jit(solution)/shard_map/ppermute | solution.py:301
  181.2 9.2 %collective-permute-start.1 = (bf16[56,2560]{1,0:T(8,128)(2,1)S(1)}, bf16[56,2560]{1,0:T(8,128)(2,1)S(1)}, u32[]{:S(2)}, u32[]{:S(2)}) collective-permute-start(bf16[56,2560]{1,0:T(8,128)(2,1)S(1)} %collective-permute-done.refs_0_), channel_id=1, source_target_pairs={{0,2},{1,3},{2,4},{3,5},{4,6},{5,7},{6,8},{7,9},{8,10},{9,11},{10,... | collective-permute-start | bytes 860168 | tf_op jit(solution)/shard_map/ppermute | solution.py:314
  187.3 9.4 %collective-permute-start.62 = (bf16[160,896]{1,0:T(8,128)(2,1)S(1)}, bf16[160,896]{1,0:T(8,128)(2,1)S(1)}, u32[]{:S(2)}, u32[]{:S(2)}) collective-permute-start(bf16[160,896]{1,0:T(8,128)(2,1)S(1)} %collective-permute-done.61.refs_0_), channel_id=1, source_target_pairs={{0,2},{1,3},{2,4},{3,5},{4,6},{5,7},{6,8},{7,9},{8,10},{9,11},{10,... | collective-permute-start | bytes 860168 | tf_op jit(solution)/shard_map/ppermute | solution.py:314
  193.3 9.5 %collective-permute-start.32 = (bf16[56,2560]{1,0:T(8,128)(2,1)S(1)}, bf16[56,2560]{1,0:T(8,128)(2,1)S(1)}, u32[]{:S(2)}, u32[]{:S(2)}) collective-permute-start(bf16[56,2560]{1,0:T(8,128)(2,1)S(1)} %collective-permute-done.31.refs_0_), channel_id=1, source_target_pairs={{0,2},{1,3},{2,4},{3,5},{4,6},{5,7},{6,8},{7,9},{8,10},{9,11},{10,... | collective-permute-start | bytes 860168 | tf_op jit(solution)/shard_map/ppermute | solution.py:314
  199.8 9.2 %collective-permute-start.2 = (bf16[56,2560]{1,0:T(8,128)(2,1)S(1)}, bf16[56,2560]{1,0:T(8,128)(2,1)S(1)}, u32[]{:S(2)}, u32[]{:S(2)}) collective-permute-start(bf16[56,2560]{1,0:T(8,128)(2,1)S(1)} %collective-permute-done.1.refs_0_), channel_id=1, source_target_pairs={{0,2},{1,3},{2,4},{3,5},{4,6},{5,7},{6,8},{7,9},{8,10},{9,11},{10,... | collective-permute-start | bytes 860168 | tf_op jit(solution)/shard_map/ppermute | solution.py:314
  205.9 9.3 %collective-permute-start.63 = (bf16[160,896]{1,0:T(8,128)(2,1)S(1)}, bf16[160,896]{1,0:T(8,128)(2,1)S(1)}, u32[]{:S(2)}, u32[]{:S(2)}) collective-permute-start(bf16[160,896]{1,0:T(8,128)(2,1)S(1)} %collective-permute-done.62.refs_0_), channel_id=1, source_target_pairs={{0,2},{1,3},{2,4},{3,5},{4,6},{5,7},{6,8},{7,9},{8,10},{9,11},{10,... | collective-permute-start | bytes 860168 | tf_op jit(solution)/shard_map/ppermute | solution.py:314
  212.1 9.6 %collective-permute-start.33 = (bf16[56,2560]{1,0:T(8,128)(2,1)S(1)}, bf16[56,2560]{1,0:T(8,128)(2,1)S(1)}, u32[]{:S(2)}, u32[]{:S(2)}) collective-permute-start(bf16[56,2560]{1,0:T(8,128)(2,1)S(1)} %collective-permute-done.32.refs_0_), channel_id=1, source_target_pairs={{0,2},{1,3},{2,4},{3,5},{4,6},{5,7},{6,8},{7,9},{8,10},{9,11},{10,... | collective-permute-start | bytes 860168 | tf_op jit(solution)/shard_map/ppermute | solution.py:314
  218.3 9.5 %collective-permute-start.3 = (bf16[56,2560]{1,0:T(8,128)(2,1)S(1)}, bf16[56,2560]{1,0:T(8,128)(2,1)S(1)}, u32[]{:S(2)}, u32[]{:S(2)}) collective-permute-start(bf16[56,2560]{1,0:T(8,128)(2,1)S(1)} %collective-permute-done.2.refs_0_), channel_id=1, source_target_pairs={{0,2},{1,3},{2,4},{3,5},{4,6},{5,7},{6,8},{7,9},{8,10},{9,11},{10,... | collective-permute-start | bytes 860168 | tf_op jit(solution)/shard_map/ppermute | solution.py:314
  224.5 9.4 %collective-permute-start.64 = (bf16[160,896]{1,0:T(8,128)(2,1)S(1)}, bf16[160,896]{1,0:T(8,128)(2,1)S(1)}, u32[]{:S(2)}, u32[]{:S(2)}) collective-permute-start(bf16[160,896]{1,0:T(8,128)(2,1)S(1)} %collective-permute-done.63.refs_0_), channel_id=1, source_target_pairs={{0,2},{1,3},{2,4},{3,5},{4,6},{5,7},{6,8},{7,9},{8,10},{9,11},{10,... | collective-permute-start | bytes 860168 | tf_op jit(solution)/shard_map/ppermute | solution.py:314
  231.1 9.3 %collective-permute-start.34 = (bf16[56,2560]{1,0:T(8,128)(2,1)S(1)}, bf16[56,2560]{1,0:T(8,128)(2,1)S(1)}, u32[]{:S(2)}, u32[]{:S(2)}) collective-permute-start(bf16[56,2560]{1,0:T(8,128)(2,1)S(1)} %collective-permute-done.33.refs_0_), channel_id=1, source_target_pairs={{0,2},{1,3},{2,4},{3,5},{4,6},{5,7},{6,8},{7,9},{8,10},{9,11},{10,... | collective-permute-start | bytes 860168 | tf_op jit(solution)/shard_map/ppermute | solution.py:314
  238.7 9.1 %collective-permute-start.4 = (bf16[56,2560]{1,0:T(8,128)(2,1)S(1)}, bf16[56,2560]{1,0:T(8,128)(2,1)S(1)}, u32[]{:S(2)}, u32[]{:S(2)}) collective-permute-start(bf16[56,2560]{1,0:T(8,128)(2,1)S(1)} %collective-permute-done.3.refs_0_), channel_id=1, source_target_pairs={{0,2},{1,3},{2,4},{3,5},{4,6},{5,7},{6,8},{7,9},{8,10},{9,11},{10,... | collective-permute-start | bytes 860168 | tf_op jit(solution)/shard_map/ppermute | solution.py:314
  244.7 9.3 %collective-permute-start.65 = (bf16[160,896]{1,0:T(8,128)(2,1)S(1)}, bf16[160,896]{1,0:T(8,128)(2,1)S(1)}, u32[]{:S(2)}, u32[]{:S(2)}) collective-permute-start(bf16[160,896]{1,0:T(8,128)(2,1)S(1)} %collective-permute-done.64.refs_0_), channel_id=1, source_target_pairs={{0,2},{1,3},{2,4},{3,5},{4,6},{5,7},{6,8},{7,9},{8,10},{9,11},{10,... | collective-permute-start | bytes 860168 | tf_op jit(solution)/shard_map/ppermute | solution.py:314
  248.3 8.8 %collective-permute-start.48 = (bf16[56,2560]{1,0:T(8,128)(2,1)S(1)}, bf16[56,2560]{1,0:T(8,128)(2,1)S(1)}, u32[]{:S(2)}, u32[]{:S(2)}) collective-permute-start(bf16[56,2560]{1,0:T(8,128)(2,1)S(1)} %collective-permute-done.34.refs_0_), channel_id=1, source_target_pairs={{0,1},{1,0},{2,3},{3,2},{4,5},{5,4},{6,7},{7,6},{8,9},{9,8},{10,11... | collective-permute-start | bytes 860168 | tf_op jit(solution)/shard_map/ppermute | solution.py:301
  251.5 9.1 %collective-permute-start.35 = (bf16[56,2560]{1,0:T(8,128)(2,1)S(1)}, bf16[56,2560]{1,0:T(8,128)(2,1)S(1)}, u32[]{:S(2)}, u32[]{:S(2)}) collective-permute-start(bf16[56,2560]{1,0:T(8,128)(2,1)S(1)} %collective-permute-done.34.refs_0_), channel_id=1, source_target_pairs={{0,2},{1,3},{2,4},{3,5},{4,6},{5,7},{6,8},{7,9},{8,10},{9,11},{10,... | collective-permute-start | bytes 860168 | tf_op jit(solution)/shard_map/ppermute | solution.py:314
  258.5 9.1 %collective-permute-start.5 = (bf16[56,2560]{1,0:T(8,128)(2,1)S(1)}, bf16[56,2560]{1,0:T(8,128)(2,1)S(1)}, u32[]{:S(2)}, u32[]{:S(2)}) collective-permute-start(bf16[56,2560]{1,0:T(8,128)(2,1)S(1)} %collective-permute-done.4.refs_0_), channel_id=1, source_target_pairs={{0,2},{1,3},{2,4},{3,5},{4,6},{5,7},{6,8},{7,9},{8,10},{9,11},{10,... | collective-permute-start | bytes 860168 | tf_op jit(solution)/shard_map/ppermute | solution.py:314
  260.6 8.7 %collective-permute-start.12 = (bf16[56,2560]{1,0:T(8,128)(2,1)S(1)}, bf16[56,2560]{1,0:T(8,128)(2,1)S(1)}, u32[]{:S(2)}, u32[]{:S(2)}) collective-permute-start(bf16[56,2560]{1,0:T(8,128)(2,1)S(1)} %collective-permute-done.11.refs_1_), channel_id=1, source_target_pairs={{0,14},{1,15},{2,0},{3,1},{4,2},{5,3},{6,4},{7,5},{8,6},{9,7},{10,... | collective-permute-start | bytes 860168 | tf_op jit(solution)/shard_map/ppermute | solution.py:314
  265.2 9.1 %collective-permute-start.66 = (bf16[160,896]{1,0:T(8,128)(2,1)S(1)}, bf16[160,896]{1,0:T(8,128)(2,1)S(1)}, u32[]{:S(2)}, u32[]{:S(2)}) collective-permute-start(bf16[160,896]{1,0:T(8,128)(2,1)S(1)} %collective-permute-done.65.refs_0_), channel_id=1, source_target_pairs={{0,2},{1,3},{2,4},{3,5},{4,6},{5,7},{6,8},{7,9},{8,10},{9,11},{10,... | collective-permute-start | bytes 860168 | tf_op jit(solution)/shard_map/ppermute | solution.py:314
  271.8 9.2 %collective-permute-start.36 = (bf16[56,2560]{1,0:T(8,128)(2,1)S(1)}, bf16[56,2560]{1,0:T(8,128)(2,1)}, u32[]{:S(2)}, u32[]{:S(2)}) collective-permute-start(bf16[56,2560]{1,0:T(8,128)(2,1)S(1)} %collective-permute-done.35.refs_0_), channel_id=1, source_target_pairs={{0,2},{1,3},{2,4},{3,5},{4,6},{5,7},{6,8},{7,9},{8,10},{9,11},{10,... | collective-permute-start | bytes 860168 | tf_op jit(solution)/shard_map/ppermute | solution.py:314
  276.0 8.9 %collective-permute-start.16 = (bf16[56,2560]{1,0:T(8,128)(2,1)S(1)}, bf16[56,2560]{1,0:T(8,128)(2,1)S(1)}, u32[]{:S(2)}, u32[]{:S(2)}) collective-permute-start(bf16[56,2560]{1,0:T(8,128)(2,1)S(1)} %collective-permute-done.5.refs_0_), channel_id=1, source_target_pairs={{0,1},{1,0},{2,3},{3,2},{4,5},{5,4},{6,7},{7,6},{8,9},{9,8},{10,11... | collective-permute-start | bytes 860168 | tf_op jit(solution)/shard_map/ppermute | solution.py:301
  278.5 9.2 %collective-permute-start.6 = (bf16[56,2560]{1,0:T(8,128)(2,1)S(1)}, bf16[56,2560]{1,0:T(8,128)(2,1)}, u32[]{:S(2)}, u32[]{:S(2)}) collective-permute-start(bf16[56,2560]{1,0:T(8,128)(2,1)S(1)} %collective-permute-done.5.refs_0_), channel_id=1, source_target_pairs={{0,2},{1,3},{2,4},{3,5},{4,6},{5,7},{6,8},{7,9},{8,10},{9,11},{10,... | collective-permute-start | bytes 860168 | tf_op jit(solution)/shard_map/ppermute | solution.py:314
  285.6 38.8 %collective-permute-start.75 = (bf16[160,896]{1,0:T(8,128)(2,1)}, bf16[160,896]{1,0:T(8,128)(2,1)}, u32[]{:S(2)}, u32[]{:S(2)}) collective-permute-start(bf16[160,896]{1,0:T(8,128)(2,1)} %collective-permute-done.73.refs_1_), channel_id=1, source_target_pairs={{0,1},{1,0},{2,3},{3,2},{4,5},{5,4},{6,7},{7,6},{8,9},{9,8},{10,11... | collective-permute-start | bytes 860168 | tf_op jit(solution)/shard_map/ppermute | solution.py:301
  286.3 40.6 %collective-permute-start.44 = (bf16[56,2560]{1,0:T(8,128)(2,1)}, bf16[56,2560]{1,0:T(8,128)(2,1)}, u32[]{:S(2)}, u32[]{:S(2)}) collective-permute-start(bf16[56,2560]{1,0:T(8,128)(2,1)} %collective-permute-done.36.refs_0_), channel_id=1, source_target_pairs={{0,1},{1,0},{2,3},{3,2},{4,5},{5,4},{6,7},{7,6},{8,9},{9,8},{10,11... | collective-permute-start | bytes 860168 | tf_op jit(solution)/shard_map/ppermute | solution.py:301
  287.7 39.2 %collective-permute-start.45 = (bf16[56,2560]{1,0:T(8,128)(2,1)}, bf16[56,2560]{1,0:T(8,128)(2,1)}, u32[]{:S(2)}, u32[]{:S(2)}) collective-permute-start(bf16[56,2560]{1,0:T(8,128)(2,1)} %collective-permute-done.43.refs_1_), channel_id=1, source_target_pairs={{0,1},{1,0},{2,3},{3,2},{4,5},{5,4},{6,7},{7,6},{8,9},{9,8},{10,11... | collective-permute-start | bytes 860168 | tf_op jit(solution)/shard_map/ppermute | solution.py:301
  289.0 40.1 %collective-permute-start.14 = (bf16[56,2560]{1,0:T(8,128)(2,1)}, bf16[56,2560]{1,0:T(8,128)(2,1)}, u32[]{:S(2)}, u32[]{:S(2)}) collective-permute-start(bf16[56,2560]{1,0:T(8,128)(2,1)} %collective-permute-done.6.refs_0_), channel_id=1, source_target_pairs={{0,1},{1,0},{2,3},{3,2},{4,5},{5,4},{6,7},{7,6},{8,9},{9,8},{10,11... | collective-permute-start | bytes 860168 | tf_op jit(solution)/shard_map/ppermute | solution.py:301
  291.1 38.1 %collective-permute-start.15 = (bf16[56,2560]{1,0:T(8,128)(2,1)}, bf16[56,2560]{1,0:T(8,128)(2,1)}, u32[]{:S(2)}, u32[]{:S(2)}) collective-permute-start(bf16[56,2560]{1,0:T(8,128)(2,1)} %collective-permute-done.13.refs_1_), channel_id=1, source_target_pairs={{0,1},{1,0},{2,3},{3,2},{4,5},{5,4},{6,7},{7,6},{8,9},{9,8},{10,11... | collective-permute-start | bytes 860168 | tf_op jit(solution)/shard_map/ppermute | solution.py:301
  (136 other events, 655.4 us)
